TPU v7x, 32 devices: a whole 2x2x4 slice. The times are simulated.
32 devices in a mesh: af: 4 (over y, x), sa: 8 (over z, core).
Axes of the slice: x: 2, y: 2, z: 4, core: 2. Of those that a mesh axis runs over, the one named last changes fastest.
Arguments:
- data_real: bfloat16 [64, 512, 512], P('af', 'sa'), may hold values from -0.5 to 0.5
- data_imaginary: bfloat16 [64, 512, 512], P('af', 'sa'), may hold values from -0.5 to 0.5
- wavelet_real: float32 [64], P('af'), may hold values from -2.5 to 2.5
- wavelet_imaginary: float32 [64], P('af'), may hold values from -2.5 to 2.5
- primaries_real: float32 [64, 512, 512], P('af', 'sa'), may hold values from -3 to 3
- primaries_imaginary: float32 [64, 512, 512], P('af', 'sa'), may hold values from -3 to 3
Outputs:
- updated_real: float32 [64, 512, 512], P('af', 'sa')
- updated_imaginary: float32 [64, 512, 512], P('af', 'sa')
- misfit: float32 [2], replicated
All inputs are finite; a program needn't handle non-finite values.
Results may differ from a plain program's by a relative error of at most 0.0018.
Values may be sent and summed in bfloat16 or wider, within the bound.
A program may use at most 128 MiB of HBM per device.

v0:
```python
import functools
import math

import jax
import jax.numpy as jnp
from jax import lax
from jax.experimental import pallas as pl
from jax.experimental.pallas import tpu as pltpu
from jax.sharding import PartitionSpec as P

ITERS = 2
STEP_LENGTH = 0.02
THRESHOLD = 0.25
CHUNKS = 2
WIRE = jnp.float16
LARGEST = 60000.0
GROUP = 8
HALF = math.sqrt(0.5)
MESH = pl.DeviceIdType.MESH


def product_kernel(first, offset, wr_ref, wi_ref, whole_ref, own_r_ref, own_i_ref, *rest):
    if first:
        gr_ref, gi_ref, out_ref, sum_ref = rest
        gr = gr_ref[0]
        gi = gi_ref[0]
    else:
        g_ref, gi_ref, out_ref, sum_ref = rest
        parts = g_ref.shape[0]
        gr = jnp.concatenate([g_ref[a, 0] for a in range(parts)], axis=1)
        gi = jnp.concatenate([gi_ref[a, 0] for a in range(parts)], axis=1)
    at = pl.program_id(0) + offset
    qr = wr_ref[at]
    qi = wi_ref[at]
    rows = gr.shape[0]
    n = gr.shape[1]
    whole_r = whole_ref[:, 0, 0].reshape(n, n)
    whole_i = whole_ref[:, 1, 0].reshape(n, n)
    left = jnp.concatenate([gr.astype(jnp.bfloat16), gi.astype(jnp.bfloat16)], axis=0)
    pr = jnp.dot(left, whole_r, preferred_element_type=jnp.float32)
    pi = jnp.dot(left, whole_i, preferred_element_type=jnp.float32)
    er = own_r_ref[0].astype(jnp.float32) + (pr[:rows] - pi[rows:]) - (qr * gr - qi * gi)
    ei = own_i_ref[0].astype(jnp.float32) + (pi[:rows] + pr[rows:]) - (qr * gi + qi * gr)
    sum_ref[0] = jnp.sum(er * er + ei * ei, axis=0, keepdims=True)
    eb = jnp.concatenate([er.astype(jnp.bfloat16), ei.astype(jnp.bfloat16)], axis=0)
    dims = (((1,), (1,)), ((), ()))
    br = lax.dot_general(eb, whole_r, dims, preferred_element_type=jnp.float32)
    bi = lax.dot_general(eb, whole_i, dims, preferred_element_type=jnp.float32)
    hr = qr * er + qi * ei - (br[:rows] + bi[rows:])
    hi = qr * ei - qi * er - (br[rows:] - bi[:rows])
    zr = gr + STEP_LENGTH * hr
    zi = gi + STEP_LENGTH * hi
    parts = out_ref.shape[0]
    width = n // parts
    for a in range(parts):
        out_ref[a, 0, 0] = zr[:, a * width : (a + 1) * width]
        out_ref[a, 1, 0] = zi[:, a * width : (a + 1) * width]


def product(offset, count, local, parts, wr, wi, whole, own_r, own_i, current):
    sa, _, _, rows, n = whole.shape
    first = len(current) == 2
    plain = pl.BlockSpec((1, rows, n), lambda f: (f + offset, 0, 0))
    scalars = pl.BlockSpec(memory_space=pltpu.SMEM)
    width = n // parts
    if first:
        cur_specs = [plain, plain]
    else:
        block = (parts, 1, rows, width)
        cur_specs = [
            pl.BlockSpec(block, lambda f: (0, f + offset, 0, 0)),
            pl.BlockSpec(block, lambda f: (0, f + offset + local, 0, 0)),
        ]
        current = (current[0], current[0])
    return pl.pallas_call(
        functools.partial(product_kernel, first, offset),
        grid=(count,),
        in_specs=[scalars, scalars, pl.BlockSpec((sa, 2, 1, rows, n), lambda f: (0, 0, f, 0, 0)), plain, plain]
        + cur_specs,
        out_specs=[
            pl.BlockSpec((parts, 2, 1, rows, width), lambda f: (0, 0, f, 0, 0)),
            pl.BlockSpec((1, 1, n), lambda f: (f, 0, 0)),
        ],
        out_shape=[
            jax.ShapeDtypeStruct((parts, 2, count, rows, width), jnp.float32),
            jax.ShapeDtypeStruct((count, 1, n), jnp.float32),
        ],
        cost_estimate=pl.CostEstimate(
            flops=16 * count * rows * n * n, bytes_accessed=count * n * (n * 4 + rows * 20), transcendentals=0
        ),
        compiler_params=pltpu.CompilerParams(vmem_limit_bytes=60 * 2**20),
    )(wr, wi, whole, own_r, own_i, *current)


def add(a, b):
    return (a[0] + b[0], a[1] + b[1])


def sub(a, b):
    return (a[0] - b[0], a[1] - b[1])


def turn(a, sign):
    return (-a[1], a[0]) if sign > 0 else (a[1], -a[0])


def rotate(a, turns):
    c, s = math.cos(2 * math.pi * turns), math.sin(2 * math.pi * turns)
    return (a[0] * c - a[1] * s, a[0] * s + a[1] * c)


def four(a, b, c, d, sign):
    s0, s1, s2, s3 = add(a, c), sub(a, c), add(b, d), turn(sub(b, d), sign)
    return add(s0, s2), add(s1, s3), sub(s0, s2), sub(s1, s3)


def eight(x, sign):
    even = four(x[0], x[2], x[4], x[6], sign)
    odd = four(x[1], x[3], x[5], x[7], sign)
    o1 = add(odd[1], turn(odd[1], sign))
    o3 = sub(turn(odd[3], sign), odd[3])
    odd = (odd[0], (o1[0] * HALF, o1[1] * HALF), turn(odd[2], sign), (o3[0] * HALF, o3[1] * HALF))
    return [add(even[k], odd[k]) for k in range(4)] + [sub(even[k], odd[k]) for k in range(4)]


def shrink(v):
    return v - jnp.clip(v, -THRESHOLD, THRESHOLD)


def transform_kernel(pieces, bound, *refs):
    scale_ref, in_refs, out_ref, work = refs[0], refs[1 : pieces + 1], refs[pieces + 1], refs[pieces + 2]
    parts, slots, block, width = out_ref.shape
    local = slots // 2
    piece = local // pieces
    radix = 8
    in_scale = scale_ref[0] / radix
    out_scale = scale_ref[1] / radix

    def one(g, _):
        at = pl.ds(pl.multiple_of(g * GROUP, GROUP), GROUP)

        def load(f):
            a, b = divmod(f, local)
            c, d = divmod(b, piece)
            ref = in_refs[c]
            return (
                ref[a, 0, d, at, :].astype(jnp.float32) * in_scale,
                ref[a, 1, d, at, :].astype(jnp.float32) * in_scale,
            )

        for f1 in range(radix):
            y = eight([load(f1 + radix * f2) for f2 in range(radix)], 1)
            for t2 in range(radix):
                v = rotate(y[t2], f1 * t2 / 64) if f1 * t2 else y[t2]
                work[0, radix * f1 + t2] = v[0]
                work[1, radix * f1 + t2] = v[1]
        for t2 in range(radix):
            y = eight([(work[0, radix * f1 + t2], work[1, radix * f1 + t2]) for f1 in range(radix)], 1)
            y = [(shrink(v[0]), shrink(v[1])) for v in y]
            y = eight(y, -1)
            for f1 in range(radix):
                v = rotate(y[f1], -f1 * t2 / 64) if f1 * t2 else y[f1]
                work[0, radix * f1 + t2] = v[0]
                work[1, radix * f1 + t2] = v[1]
        largest = jnp.zeros((GROUP, width), jnp.float32)
        for f1 in range(radix):
            y = eight([(work[0, radix * f1 + t2], work[1, radix * f1 + t2]) for t2 in range(radix)], -1)
            for f2 in range(radix):
                a, b = divmod(f1 + radix * f2, local)
                re, im = y[f2][0] * out_scale, y[f2][1] * out_scale
                out_ref[a, b, at, :] = re
                out_ref[a, b + local, at, :] = im
                if bound:
                    largest = jnp.maximum(largest, jnp.maximum(jnp.abs(re), jnp.abs(im)))
        if bound:
            for a in range(parts):
                out_ref[a, 2 * local, at, :] = largest
        return 0

    lax.fori_loop(0, block // GROUP, one, 0)


def transform(arrays, in_scale, out_scale, bound):
    pieces = len(arrays)
    parts, _, piece, rows, width = arrays[0].shape
    local = piece * pieces
    block = min(16, rows)
    slots = 2 * local + (1 if bound else 0)
    scales = jnp.stack([jnp.float32(in_scale), jnp.float32(out_scale)])
    return pl.pallas_call(
        functools.partial(transform_kernel, pieces, bound),
        grid=(rows // block,),
        in_specs=[pl.BlockSpec(memory_space=pltpu.SMEM)]
        + [pl.BlockSpec((parts, 2, piece, block, width), lambda r: (0, 0, 0, r, 0))] * pieces,
        out_specs=pl.BlockSpec((parts, slots, block, width), lambda r: (0, 0, r, 0)),
        out_shape=jax.ShapeDtypeStruct((parts, slots, rows, width), jnp.float32),
        scratch_shapes=[pltpu.VMEM((2, parts * local, GROUP, width), jnp.float32)],
        cost_estimate=pl.CostEstimate(
            flops=4000 * rows * width, bytes_accessed=16 * parts * local * rows * width, transcendentals=0
        ),
        compiler_params=pltpu.CompilerParams(vmem_limit_bytes=60 * 2**20),
    )(scales, *arrays)


def total_kernel(counts, own_ref, out_ref, slots, send_sem, recv_sem):
    afs, sas = counts
    n = afs * sas
    me = lax.axis_index("af") * sas + lax.axis_index("sa")

    def peer(k):
        p = lax.rem(me + k, n)
        return (p // sas, lax.rem(p, sas))

    def hello(k, _):
        pl.semaphore_signal(barrier, inc=1, device_id=peer(k), device_id_type=MESH)
        return 0

    def copy(k):
        return pltpu.make_async_remote_copy(
            src_ref=own_ref,
            dst_ref=slots.at[k],
            send_sem=send_sem.at[k],
            recv_sem=recv_sem.at[k],
            device_id=peer(k),
            device_id_type=MESH,
        )

    def start(k, _):
        copy(k).start()
        return 0

    def finish(k, value):
        copy(k).wait()
        return value + slots[k]

    barrier = pltpu.get_barrier_semaphore()
    lax.fori_loop(1, n, hello, 0)
    pl.semaphore_wait(barrier, n - 1)
    lax.fori_loop(1, n, start, 0)
    out_ref[...] = lax.fori_loop(1, n, finish, own_ref[...])


def total(own, counts):
    n = counts[0] * counts[1]
    return pl.pallas_call(
        functools.partial(total_kernel, counts),
        out_shape=jax.ShapeDtypeStruct(own.shape, own.dtype),
        in_specs=[pl.BlockSpec(memory_space=pltpu.VMEM)],
        out_specs=pl.BlockSpec(memory_space=pltpu.VMEM),
        scratch_shapes=[
            pltpu.VMEM((n, *own.shape), own.dtype),
            pltpu.SemaphoreType.DMA((n,)),
            pltpu.SemaphoreType.DMA((n,)),
        ],
        compiler_params=pltpu.CompilerParams(collective_id=0, has_side_effects=True),
    )(own)


def exchange(values):
    return lax.all_to_all(values, "af", split_axis=0, concat_axis=0, tiled=True)


def join_kernel(scale_ref, re_ref, im_ref, out_re, out_im):
    parts, _, _, width = re_ref.shape
    scale = scale_ref[0]
    for a in range(parts):
        cut = slice(a * width, (a + 1) * width)
        out_re[:, :, cut] = re_ref[a] * scale
        out_im[:, :, cut] = im_ref[a] * scale


def join(current, scale, local):
    parts, _, rows, width = current.shape
    count = max(1, local // 4)
    out = jax.ShapeDtypeStruct((local, rows, parts * width), jnp.float32)
    out_spec = pl.BlockSpec((count, rows, parts * width), lambda f: (f, 0, 0))
    block = (parts, count, rows, width)
    steps = local // count
    return pl.pallas_call(
        join_kernel,
        grid=(steps,),
        in_specs=[
            pl.BlockSpec(memory_space=pltpu.SMEM),
            pl.BlockSpec(block, lambda f: (0, f, 0, 0)),
            pl.BlockSpec(block, lambda f: (0, f + steps, 0, 0)),
        ],
        out_specs=[out_spec, out_spec],
        out_shape=[out, out],
        compiler_params=pltpu.CompilerParams(vmem_limit_bytes=60 * 2**20),
    )(scale.reshape(1), current, current)


def on_device(counts, data_real, data_imaginary, wave_real, wave_imaginary, primaries_real, primaries_imaginary):
    parts = counts[0]
    local, rows, n = data_real.shape
    freqs = local * parts
    size = local // CHUNKS
    wholes = []
    for c in range(CHUNKS):
        cut = slice(c * size, (c + 1) * size)
        both = jnp.stack([data_real[cut], data_imaginary[cut]])
        wholes.append(lax.all_gather(both, "sa", axis=0))
    gain = 1.01 * (2 * 2.5 + n)
    spread = 1.01 * math.sqrt(2 * freqs)

    def stepped_bound(g):
        return g + STEP_LENGTH * gain * (0.5 + gain * g)

    z_scale = 1.0
    z_bound = stepped_bound(3.0)
    sums = []
    current = (primaries_real, primaries_imaginary)
    for iteration in range(ITERS):
        last = iteration == ITERS - 1
        traces = [None] * CHUNKS
        squares = []
        for c in range(CHUNKS):
            stepped, square = product(
                c * size, size, local, parts, wave_real, wave_imaginary, wholes[c], data_real, data_imaginary, current,
            )
            squares.append(square)
            traces[c] = exchange((stepped * (1.0 / z_scale)).astype(WIRE)).astype(jnp.float32)
        sums.append(jnp.sum(jnp.concatenate(squares)))
        g_scale = spread * z_bound / LARGEST
        back = transform(traces, z_scale, 1.0 / g_scale, not last)
        moved = exchange(back.astype(WIRE)).astype(jnp.float32)
        if last:
            updated = join(moved, jnp.float32(g_scale), local)
        else:
            g_bound = 1.002 * g_scale * jnp.max(moved[:, 2 * local]) + 1e-6
            current = (moved * g_scale,)
            z_bound = stepped_bound(g_bound)
            z_scale = z_bound / LARGEST
    row = lax.broadcasted_iota(jnp.int32, (8, 128), 0)
    own = jnp.where(row == 0, sums[0], jnp.where(row == 1, sums[1], 0.0))
    misfit = total(own, counts)[:ITERS, 0] / (freqs * n * n)
    return (updated[0], updated[1], misfit)


def solution(mesh):
    split = P("af", "sa", None)
    counts = (mesh.shape["af"], mesh.shape["sa"])
    return jax.shard_map(
        functools.partial(on_device, counts),
        mesh=mesh,
        in_specs=(split, split, P("af"), P("af"), split, split),
        out_specs=(split, split, P()),
        check_vma=False,
    )
```

profile of v0, /device:TPU:0, one launch (start us, length us, event | category | flops | bytes accessed | tf_op | source)
XLA Modules:
  0.0 357.5 jit_solution(11176112081411550915)
XLA Ops:
  11.1 83.8 %all-gather.7.cloned.1.call-done = bf16[16,8,64,512]{3,2,1,0:T(8,128)(2,1)} async-done(((bf16[2,8,64,512]{3,2,1,0:T(8,128)(2,1)}), bf16[16,8,64,512]{3,2,1,0:T(8,128)(2,1)}) %all-gather.7.cloned.1.call-update) | async-done | bytes 8388624 | tf_op jit(solution)/shard_map/all_gather | solution.py:302
  94.9 10.5 %shard_map.86 = (f32[4,2,8,64,128]{4,3,2,1,0:T(8,128)}, f32[8,1,512]{2,1,0:T(1,128)}) custom-call(f32[16]{0:T(128)} %wr_ref.7, f32[16]{0:T(128)} %wi_ref.7, bf16[8,2,8,64,512]{4,3,2,1,0:T(8,128)(2,1)} %bitcast.13, bf16[16,64,512]{2,1,0:T(8,128)(2,1)} %own_r_ref.7, bf16[16,64,512]{2,1,0:T(8,128)(2,1)} %own_i_ref.7, f32[16,64,512]{2,1,0:T(8,128)} %rest_0_.3, ...), custom_call_target="tpu_custom_call" | custom-call | flops 2147483648 | bytes 13631488 | tf_op jit(solution)/shard_map/pallas_call | solution.py:75
  105.4 2.9 convert_element_type.38
  108.3 3.7 %all-to-all-start.1 = ((f16[4,2,8,64,128]{4,3,2,1,0:T(8,128)(2,1)}), f16[4,2,8,64,128]{4,3,2,1,0:T(8,128)(2,1)S(1)}, u32[]{:S(2)}, u32[]{:S(2)}) async-start(f16[4,2,8,64,128]{4,3,2,1,0:T(8,128)(2,1)} %convert_element_type.38), calls=%async_computation.1 | async-start | bytes 2097152 | tf_op jit(solution)/shard_map/all_to_all | solution.py:260
  112.0 65.6 %all-gather.5.cloned.1.call-done = bf16[16,8,64,512]{3,2,1,0:T(8,128)(2,1)} async-done(((bf16[2,8,64,512]{3,2,1,0:T(8,128)(2,1)}), bf16[16,8,64,512]{3,2,1,0:T(8,128)(2,1)}) %all-gather.5.cloned.1.call-update) | async-done | bytes 8388624 | tf_op jit(solution)/shard_map/all_gather | solution.py:302
  177.7 10.3 %shard_map.85 = (f32[4,2,8,64,128]{4,3,2,1,0:T(8,128)}, f32[8,1,512]{2,1,0:T(1,128)}) custom-call(f32[16]{0:T(128)} %wr_ref.7, f32[16]{0:T(128)} %wi_ref.7, bf16[8,2,8,64,512]{4,3,2,1,0:T(8,128)(2,1)} %bitcast.15, bf16[16,64,512]{2,1,0:T(8,128)(2,1)} %own_r_ref.7, bf16[16,64,512]{2,1,0:T(8,128)(2,1)} %own_i_ref.7, f32[16,64,512]{2,1,0:T(8,128)} %rest_0_.3, ...), custom_call_target="tpu_custom_call" | custom-call | flops 2147483648 | bytes 13631488 | tf_op jit(solution)/shard_map/pallas_call | solution.py:75
  188.0 2.9 convert_element_type.36
  190.9 3.6 %all-to-all-start = ((f16[4,2,8,64,128]{4,3,2,1,0:T(8,128)(2,1)}), f16[4,2,8,64,128]{4,3,2,1,0:T(8,128)(2,1)S(1)}, u32[]{:S(2)}, u32[]{:S(2)}) async-start(f16[4,2,8,64,128]{4,3,2,1,0:T(8,128)(2,1)} %convert_element_type.36), calls=%async_computation | async-start | bytes 2097152 | tf_op jit(solution)/shard_map/all_to_all | solution.py:260
  196.0 12.6 %all-to-all-done = f16[4,2,8,64,128]{4,3,2,1,0:T(8,128)(2,1)S(1)} async-done(((f16[4,2,8,64,128]{4,3,2,1,0:T(8,128)(2,1)}), f16[4,2,8,64,128]{4,3,2,1,0:T(8,128)(2,1)S(1)}, u32[]{:S(2)}, u32[]{:S(2)}) %all-to-all-start) | async-done | bytes 1048608 | tf_op jit(solution)/shard_map/all_to_all | solution.py:260
  210.2 6.8 %shard_map.87 = f32[4,33,64,128]{3,2,1,0:T(8,128)} custom-call(f32[2]{0:T(128)} %constant.4.clone.1.refs_0_, f32[4,2,8,64,128]{4,3,2,1,0:T(8,128)} %convert_element_type.37.refs_1_, f32[4,2,8,64,128]{4,3,2,1,0:T(8,128)} %convert_element_type.39.refs_2_), custom_call_target="tpu_custom_call" | custom-call | flops 32768000 | bytes 8388608 | tf_op jit(solution)/shard_map/pallas_call | solution.py:190
  216.9 2.8 convert_element_type.40
  219.8 28.4 %all_to_all.30 = f16[4,33,64,128]{3,2,1,0:T(8,128)(2,1)S(1)} all-to-all(f16[4,33,64,128]{3,2,1,0:T(8,128)(2,1)S(1)} %convert_element_type.40), channel_id=1, replica_groups=mesh['af'=4,'sa'=8] {'af'}, dimensions={0} | all-to-all | bytes 4325376 | tf_op jit(solution)/shard_map/all_to_all | solution.py:260
  252.5 10.4 %shard_map.89 = (f32[4,2,8,64,128]{4,3,2,1,0:T(8,128)}, f32[8,1,512]{2,1,0:T(1,128)}) custom-call(f32[16]{0:T(128)} %wr_ref.7, f32[16]{0:T(128)} %wi_ref.7, bf16[8,2,8,64,512]{4,3,2,1,0:T(8,128)(2,1)} %bitcast.14, bf16[16,64,512]{2,1,0:T(8,128)(2,1)} %own_r_ref.7, bf16[16,64,512]{2,1,0:T(8,128)(2,1)} %own_i_ref.7, ...), custom_call_target="tpu_custom_call" | custom-call | flops 2147483648 | bytes 13631488 | tf_op jit(solution)/shard_map/pallas_call | solution.py:75
  263.0 2.9 multiply_convert_fusion
  265.8 3.5 all-to-all-start.4
  269.4 10.4 %shard_map.88 = (f32[4,2,8,64,128]{4,3,2,1,0:T(8,128)}, f32[8,1,512]{2,1,0:T(1,128)}) custom-call(f32[16]{0:T(128)} %wr_ref.7, f32[16]{0:T(128)} %wi_ref.7, bf16[8,2,8,64,512]{4,3,2,1,0:T(8,128)(2,1)} %bitcast.16, bf16[16,64,512]{2,1,0:T(8,128)(2,1)} %own_r_ref.7, bf16[16,64,512]{2,1,0:T(8,128)(2,1)} %own_i_ref.7, ...), custom_call_target="tpu_custom_call" | custom-call | flops 2147483648 | bytes 13631488 | tf_op jit(solution)/shard_map/pallas_call | solution.py:75
  279.8 2.9 multiply_convert_fusion.1
  282.6 4.1 %all-to-all-start.3 = ((f16[4,2,8,64,128]{4,3,2,1,0:T(8,128)(2,1)}), f16[4,2,8,64,128]{4,3,2,1,0:T(8,128)(2,1)S(1)}, u32[]{:S(2)}, u32[]{:S(2)}) async-start(f16[4,2,8,64,128]{4,3,2,1,0:T(8,128)(2,1)} %multiply_convert_fusion.1), calls=%async_computation.3 | async-start | bytes 2097152 | tf_op jit(solution)/shard_map/all_to_all | solution.py:260
  288.9 9.3 %all-to-all-done.3 = f16[4,2,8,64,128]{4,3,2,1,0:T(8,128)(2,1)S(1)} async-done(((f16[4,2,8,64,128]{4,3,2,1,0:T(8,128)(2,1)}), f16[4,2,8,64,128]{4,3,2,1,0:T(8,128)(2,1)S(1)}, u32[]{:S(2)}, u32[]{:S(2)}) %all-to-all-start.3) | async-done | bytes 1048608 | tf_op jit(solution)/shard_map/all_to_all | solution.py:260
  299.7 6.7 %shard_map.90 = f32[4,32,64,128]{3,2,1,0:T(8,128)} custom-call(f32[2]{0:T(128)} %pad_maximum_fusion.2.refs_0_, f32[4,2,8,64,128]{4,3,2,1,0:T(8,128)} %convert_element_type.43.refs_1_, f32[4,2,8,64,128]{4,3,2,1,0:T(8,128)} %convert_element_type.45.refs_2_), custom_call_target="tpu_custom_call" | custom-call | flops 32768000 | bytes 8388608 | tf_op jit(solution)/shard_map/pallas_call | solution.py:190
  306.4 4.1 %convert_element_type.46 = f16[4,32,64,128]{3,2,1,0:T(8,128)(2,1)} convert(f32[4,32,64,128]{3,2,1,0:T(8,128)} %shard_map.90) | non-fusion elementwise | flops 1048576 | bytes 6291456 | tf_op jit(solution)/shard_map/convert_element_type | solution.py:326
  310.5 3.8 %all-to-all-start.5 = ((f16[4,32,64,128]{3,2,1,0:T(8,128)(2,1)}), f16[4,32,64,128]{3,2,1,0:T(8,128)(2,1)S(1)}, u32[]{:S(2)}, u32[]{:S(2)}) async-start(f16[4,32,64,128]{3,2,1,0:T(8,128)(2,1)} %convert_element_type.46), calls=%async_computation.5 | async-start | bytes 4194304 | tf_op jit(solution)/shard_map/all_to_all | solution.py:260
  320.1 22.0 %shard_map.92 = f32[8,128]{1,0:T(8,128)} custom-call(f32[8,128]{1,0:T(8,128)} %broadcast_select_fusion.own_ref), custom_call_target="tpu_custom_call" | custom-call | tf_op jit(solution)/shard_map/pallas_call | solution.py:245
  345.9 4.8 %shard_map.91 = (f32[16,64,512]{2,1,0:T(8,128)}, f32[16,64,512]{2,1,0:T(8,128)}) custom-call(f32[1]{0:T(128)} %bitcast.6.scale_ref, f32[4,32,64,128]{3,2,1,0:T(8,128)} %convert_element_type.47.re_ref.im_ref, f32[4,32,64,128]{3,2,1,0:T(8,128)} %convert_element_type.47.re_ref.im_ref), custom_call_target="tpu_custom_call" | custom-call | tf_op jit(solution)/shard_map/pallas_call | solution.py:279
  (35 shorter events, 21.3 us)
Async XLA Ops:
  7.2 87.8 %all-gather.7.cloned.1.call-start = ((), (), s32[]{:S(2)}) async-start(), calls=%async_computation.7 | async-start | bytes 9437184 | tf_op jit(solution)/shard_map/all_gather | solution.py:302
  10.0 167.7 %all-gather.5.cloned.1.call-start = ((), (), s32[]{:S(2)}) async-start(), calls=%async_computation.6 | async-start | bytes 9437184 | tf_op jit(solution)/shard_map/all_gather | solution.py:302
  108.3 82.5 %all-to-all-start.1 = ((f16[4,2,8,64,128]{4,3,2,1,0:T(8,128)(2,1)}), f16[4,2,8,64,128]{4,3,2,1,0:T(8,128)(2,1)S(1)}, u32[]{:S(2)}, u32[]{:S(2)}) async-start(f16[4,2,8,64,128]{4,3,2,1,0:T(8,128)(2,1)} %convert_element_type.38), calls=%async_computation.1 | async-start | bytes 2097152 | tf_op jit(solution)/shard_map/all_to_all | solution.py:260
  190.9 17.8 %all-to-all-start = ((f16[4,2,8,64,128]{4,3,2,1,0:T(8,128)(2,1)}), f16[4,2,8,64,128]{4,3,2,1,0:T(8,128)(2,1)S(1)}, u32[]{:S(2)}, u32[]{:S(2)}) async-start(f16[4,2,8,64,128]{4,3,2,1,0:T(8,128)(2,1)} %convert_element_type.36), calls=%async_computation | async-start | bytes 2097152 | tf_op jit(solution)/shard_map/all_to_all | solution.py:260
  265.8 16.8 %all-to-all-start.4 = ((f16[4,2,8,64,128]{4,3,2,1,0:T(8,128)(2,1)}), f16[4,2,8,64,128]{4,3,2,1,0:T(8,128)(2,1)S(1)}, u32[]{:S(2)}, u32[]{:S(2)}) async-start(f16[4,2,8,64,128]{4,3,2,1,0:T(8,128)(2,1)} %multiply_convert_fusion), calls=%async_computation.4 | async-start | bytes 2097152 | tf_op jit(solution)/shard_map/all_to_all | solution.py:260
  282.6 15.6 %all-to-all-start.3 = ((f16[4,2,8,64,128]{4,3,2,1,0:T(8,128)(2,1)}), f16[4,2,8,64,128]{4,3,2,1,0:T(8,128)(2,1)S(1)}, u32[]{:S(2)}, u32[]{:S(2)}) async-start(f16[4,2,8,64,128]{4,3,2,1,0:T(8,128)(2,1)} %multiply_convert_fusion.1), calls=%async_computation.3 | async-start | bytes 2097152 | tf_op jit(solution)/shard_map/all_to_all | solution.py:260
  310.5 3.8 %copy-start = (f32[8,1,512]{2,1,0:T(1,128)S(1)}, f32[8,1,512]{2,1,0:T(1,128)}, u32[]{:S(2)}) copy-start(f32[8,1,512]{2,1,0:T(1,128)} %get-tuple-element.20) | copy-start | bytes 49156
  310.5 4.4 %copy-start.1 = (f32[8,1,512]{2,1,0:T(1,128)S(1)}, f32[8,1,512]{2,1,0:T(1,128)}, u32[]{:S(2)}) copy-start(f32[8,1,512]{2,1,0:T(1,128)} %get-tuple-element.19) | copy-start | bytes 49156
  310.5 6.4 %copy-start.2 = (f32[8,1,512]{2,1,0:T(1,128)S(1)}, f32[8,1,512]{2,1,0:T(1,128)}, u32[]{:S(2)}) copy-start(f32[8,1,512]{2,1,0:T(1,128)} %get-tuple-element.22) | copy-start | bytes 49156
  310.5 7.0 %copy-start.3 = (f32[8,1,512]{2,1,0:T(1,128)S(1)}, f32[8,1,512]{2,1,0:T(1,128)}, u32[]{:S(2)}) copy-start(f32[8,1,512]{2,1,0:T(1,128)} %get-tuple-element.21) | copy-start | bytes 49156
  310.5 33.0 %all-to-all-start.5 = ((f16[4,32,64,128]{3,2,1,0:T(8,128)(2,1)}), f16[4,32,64,128]{3,2,1,0:T(8,128)(2,1)S(1)}, u32[]{:S(2)}, u32[]{:S(2)}) async-start(f16[4,32,64,128]{3,2,1,0:T(8,128)(2,1)} %convert_element_type.46), calls=%async_computation.5 | async-start | bytes 4194304 | tf_op jit(solution)/shard_map/all_to_all | solution.py:260
Sparse Core Ops, SparseCore 0:
  10.1 84.7 all-gather.6
  97.1 80.5 all-gather.4
where the time goes:
time: 359 us; the launch traced here: 358 us
  waiting for transfers between devices  171 us (48%)
  Pallas kernels  81.9 us (23%)
  other arithmetic  37.9 us (11%)
  blocking collectives  28.4 us (8%)
  starting transfers between devices  18.8 us (5%)
  between operations  17.5 us (5%)
    all_gather x2, waiting for transfers between devices, on_device(): wholes.append(lax.all_gather(both, 'sa', axis=0))  149 us
    pallas_call x4, Pallas kernels, product(): pl.pallas_call(functools.partial(product_kernel, first, offset), grid=(co...  41.6 us
    all_to_all x1, blocking collectives, exchange(): return lax.all_to_all(values, 'af', split_axis=0, concat_axis=0, tiled=True)  28.4 us
    pallas_call x1, Pallas kernels, total(): pl.pallas_call(functools.partial(total_kernel, counts), out_shape=jax.Sha...  22 us
    all_to_all x5, waiting for transfers between devices, exchange(): return lax.all_to_all(values, 'af', split_axis=0, concat_axis=0, tiled=True)  21.9 us
    all_to_all x5, starting transfers between devices, exchange(): return lax.all_to_all(values, 'af', split_axis=0, concat_axis=0, tiled=True)  18.8 us
    pallas_call x2, Pallas kernels, transform(): pl.pallas_call(functools.partial(transform_kernel, pieces, bound), grid=(...  13.5 us
    convert_element_type x4, other arithmetic, on_device(): (stepped * (1.0 / z_scale)).astype(WIRE)  11.5 us
  transfers between devices with their start and end apart: 7, of which 4 were waited for; matrix products, arithmetic and copies ran while one was open for 5% of the time, Pallas kernels for 15%

commit v1 on v0

v1 whole, which is shorter than its diff:
```python
import functools
import math

import jax
import jax.numpy as jnp
import numpy as np
from jax import lax
from jax.experimental import pallas as pl
from jax.experimental.pallas import tpu as pltpu
from jax.sharding import PartitionSpec as P

ITERS = 2
STEP_LENGTH = 0.02
THRESHOLD = 0.25
RADIX = 8
HALF = math.sqrt(0.5)
REACH = 64.0
TINY = 2.0**-126
MESH = pl.DeviceIdType.MESH


def encode(x):
    y = x * (1.0 / REACH)
    return ((y * y) * (y * jnp.abs(y))).astype(jnp.bfloat16)


def decode(code):
    v = code.astype(jnp.float32)
    r = lax.rsqrt(lax.rsqrt(jnp.maximum(jnp.abs(v), TINY))) * REACH
    return jnp.where(v > 0, r, jnp.where(v < 0, -r, 0.0))


def add(a, b):
    return (a[0] + b[0], a[1] + b[1])


def sub(a, b):
    return (a[0] - b[0], a[1] - b[1])


def turn(a, sign):
    return (-a[1], a[0]) if sign > 0 else (a[1], -a[0])


def rotate(a, c, s):
    return (a[0] * c - a[1] * s, a[0] * s + a[1] * c)


def four(a, b, c, d, sign):
    s0, s1, s2, s3 = add(a, c), sub(a, c), add(b, d), turn(sub(b, d), sign)
    return add(s0, s2), add(s1, s3), sub(s0, s2), sub(s1, s3)


def eight(x, sign):
    even = four(x[0], x[2], x[4], x[6], sign)
    odd = four(x[1], x[3], x[5], x[7], sign)
    o1 = add(odd[1], turn(odd[1], sign))
    o3 = sub(turn(odd[3], sign), odd[3])
    odd = (odd[0], (o1[0] * HALF, o1[1] * HALF), turn(odd[2], sign), (o3[0] * HALF, o3[1] * HALF))
    return [add(even[k], odd[k]) for k in range(4)] + [sub(even[k], odd[k]) for k in range(4)]


def shrink(v):
    return v - jnp.clip(v, -THRESHOLD, THRESHOLD)


def loop(start, stop, body):
    def step(i, _):
        body(i)
        return 0

    lax.fori_loop(start, stop, step, 0)


def kernel(
    A, S, chunks, wr, wi, twiddle, data_r, data_i, prim_r, prim_i, out, mis,
    whole, current, initial, work, traces, hs, hr, gs, gr, squares, by_af, by_sa,
    local_sem, up_sem, down_sem, ring_sem, pair_send, pair_recv,
    init_send, init_recv, h_send, h_recv, g_send, g_recv, m_send, m_recv,
):
    C = S // 2
    U, _, R, N = data_r.shape
    W = N // A
    per = RADIX // chunks
    rows = 16 if R % 16 == 0 else 8
    a = lax.axis_index("af")
    s = lax.axis_index("sa")
    c = s // 2
    k = s % 2
    partner = c * 2 + 1 - k
    mine = pl.ds(pl.multiple_of(a * W, W), W)

    def cols(b):
        return pl.ds(pl.multiple_of(b * W, W), W)

    def ahead(j):
        return lax.rem(a + j, A)

    def behind(j):
        return lax.rem(a + A - j, A)

    barrier = pltpu.get_barrier_semaphore()
    for j in range(1, A):
        pl.semaphore_signal(barrier, inc=1, device_id=(ahead(j), s), device_id_type=MESH)
    loop(
        1, S,
        lambda j: pl.semaphore_signal(barrier, inc=1, device_id=(a, lax.rem(s + j, S)), device_id_type=MESH),
    )

    locals_ = [
        pltpu.make_async_copy(data_r, whole.at[:, :, 0, s], local_sem.at[0]),
        pltpu.make_async_copy(data_i, whole.at[:, :, 1, s], local_sem.at[1]),
        pltpu.make_async_copy(prim_r, current.at[0], local_sem.at[2]),
        pltpu.make_async_copy(prim_i, current.at[1], local_sem.at[3]),
        pltpu.make_async_copy(prim_r.at[:, :, :, mine], initial.at[0, a], local_sem.at[4]),
        pltpu.make_async_copy(prim_i.at[:, :, :, mine], initial.at[1, a], local_sem.at[5]),
    ]
    for copy in locals_:
        copy.start()
    squares[...] = jnp.zeros_like(squares)
    pl.semaphore_wait(barrier, A - 1 + S - 1)

    def shard(chip, core, h):
        return whole.at[:, pl.ds(h * per, per), :, chip * 2 + core]

    def remote(src, dst, send, recv, device):
        return pltpu.make_async_remote_copy(
            src_ref=src, dst_ref=dst, send_sem=send, recv_sem=recv, device_id=device, device_id_type=MESH
        )

    def up(chip, h):
        ref = shard(chip, k, h)
        return remote(ref, ref, up_sem.at[chip, h], ring_sem.at[chip, h], (a, lax.rem(s + 2, S)))

    def down(chip, h):
        ref = shard(chip, k, h)
        return remote(ref, ref, down_sem.at[chip, h], ring_sem.at[chip, h], (a, lax.rem(s + S - 2, S)))

    def across(chip, h):
        ref = shard(chip, k, h)
        return remote(ref, ref, pair_send.at[chip, h], pair_recv.at[chip, h], (a, partner))

    def across_in(chip, h):
        ref = shard(chip, 1 - k, h)
        return remote(ref, ref, pair_send.at[chip, h], pair_recv.at[chip, h], (a, partner))

    def initials(part, j):
        src = (prim_r, prim_i)[part]
        return remote(
            src.at[:, :, :, cols(ahead(j))], initial.at[part, a],
            init_send.at[part, j], init_recv.at[part, j], (ahead(j), s),
        )

    def initials_in(part, j):
        src = (prim_r, prim_i)[part]
        return remote(
            src.at[:, :, :, mine], initial.at[part, behind(j)],
            init_send.at[part, j], init_recv.at[part, j], (ahead(j), s),
        )

    locals_[0].wait()
    locals_[1].wait()

    def first(h):
        @pl.when(c + 1 < C)
        def _():
            up(c, h).start()

        @pl.when(c > 0)
        def _():
            down(c, h).start()

        across(c, h).start()

    loop(0, chunks, first)
    for j in range(1, A):
        for part in range(2):
            initials(part, j).start()

    def arrive(d, h):
        @pl.when(c >= d)
        def _():
            src = c - d
            up(src, h).wait_recv()
            across(src, h).start()

            @pl.when(c + 1 < C)
            def _():
                up(src, h).start()

        @pl.when(c + d < C)
        def _():
            src = c + d
            down(src, h).wait_recv()
            across(src, h).start()

            @pl.when(c > 0)
            def _():
                down(src, h).start()

    loop(1, C - 1, lambda d: loop(0, chunks, lambda h: arrive(d, h)))

    def h_copy(j, f):
        to = ahead(j)
        return remote(
            hs.at[to, :, :, f], hr.at[a, :, :, f], h_send.at[j, f], h_recv.at[j, f], (to, s)
        )

    def h_copy_in(j, f):
        return remote(
            hs.at[a, :, :, f], hr.at[behind(j), :, :, f], h_send.at[j, f], h_recv.at[j, f], (ahead(j), s)
        )

    def g_copy(it, j, f):
        to = ahead(j)
        dst = gr if it == 0 else out
        return remote(
            gs.at[to, :, :, f], dst.at[:, :, f, :, mine],
            g_send.at[it, j, f], g_recv.at[it, j, f], (to, s),
        )

    def g_copy_in(it, j, f):
        dst = gr if it == 0 else out
        return remote(
            gs.at[a, :, :, f], dst.at[:, :, f, :, cols(behind(j))],
            g_send.at[it, j, f], g_recv.at[it, j, f], (ahead(j), s),
        )

    def product(it, f):
        def one(u):
            qr = wr[u * RADIX + f]
            qi = wi[u * RADIX + f]
            if it == 0:
                re = current[0, u, f]
                im = current[1, u, f]
            else:
                re = gr[0, u, f].astype(jnp.float32)
                im = gr[1, u, f].astype(jnp.float32)
            whole_r = whole[u, f, 0].reshape(N, N)
            whole_i = whole[u, f, 1].reshape(N, N)
            left = jnp.concatenate([re.astype(jnp.bfloat16), im.astype(jnp.bfloat16)], axis=0)
            pr = jnp.dot(left, whole_r, preferred_element_type=jnp.float32)
            pi = jnp.dot(left, whole_i, preferred_element_type=jnp.float32)
            er = whole[u, f, 0, s].astype(jnp.float32) + (pr[:R] - pi[R:]) - (qr * re - qi * im)
            ei = whole[u, f, 1, s].astype(jnp.float32) + (pi[:R] + pr[R:]) - (qr * im + qi * re)
            sq = er * er + ei * ei
            part = sq[:8]
            for i in range(1, R // 8):
                part = part + sq[i * 8 : (i + 1) * 8]
            row = part[:, :128]
            for i in range(1, N // 128):
                row = row + part[:, i * 128 : (i + 1) * 128]
            squares[it] += row
            eb = jnp.concatenate([er.astype(jnp.bfloat16), ei.astype(jnp.bfloat16)], axis=0)
            dims = (((1,), (1,)), ((), ()))
            br = lax.dot_general(eb, whole_r, dims, preferred_element_type=jnp.float32)
            bi = lax.dot_general(eb, whole_i, dims, preferred_element_type=jnp.float32)
            dr = encode(STEP_LENGTH * (qr * er + qi * ei - (br[:R] + bi[R:])))
            di = encode(STEP_LENGTH * (qr * ei - qi * er - (br[R:] - bi[:R])))
            for b in range(A):
                hs[b, 0, u, f] = dr[:, b * W : (b + 1) * W]
                hs[b, 1, u, f] = di[:, b * W : (b + 1) * W]
            hr[a, 0, u, f] = hs[a, 0, u, f]
            hr[a, 1, u, f] = hs[a, 1, u, f]

        loop(0, U, one)
        for j in range(1, A):
            h_copy(j, f).start()

    def stage_in(it, f):
        for j in range(1, A):
            h_copy_in(j, f).wait_recv()

        def some(g):
            at = pl.ds(pl.multiple_of(g * rows, rows), rows)
            x = []
            for f2 in range(RADIX):
                b, u = divmod(f2, U)
                re = decode(hr[b, 0, u, f, at, :])
                im = decode(hr[b, 1, u, f, at, :])
                if it == 0:
                    re = re + initial[0, b, u, f, at, :]
                    im = im + initial[1, b, u, f, at, :]
                x.append((re * (1.0 / RADIX), im * (1.0 / RADIX)))
            y = eight(x, 1)
            for t in range(RADIX):
                v = rotate(y[t], twiddle[0, f * t], twiddle[1, f * t]) if t else y[t]
                work[0, f, t, at, :] = v[0]
                work[1, f, t, at, :] = v[1]

        loop(0, R // rows, some)

    def stage_time(it):
        def some(g):
            at = pl.ds(pl.multiple_of(g * rows, rows), rows)

            def one(t):
                y = eight([(work[0, f, t, at, :], work[1, f, t, at, :]) for f in range(RADIX)], 1)
                if it > 0:
                    y = [(v[0] + traces[0, n, t, at, :], v[1] + traces[1, n, t, at, :]) for n, v in enumerate(y)]
                y = [(shrink(v[0]), shrink(v[1])) for v in y]
                if it < ITERS - 1:
                    for n, v in enumerate(y):
                        traces[0, n, t, at, :] = v[0]
                        traces[1, n, t, at, :] = v[1]
                y = eight(y, -1)
                for f in range(RADIX):
                    v = rotate(y[f], twiddle[0, f * t], -twiddle[1, f * t]) if f else y[f]
                    work[0, f, t, at, :] = v[0]
                    work[1, f, t, at, :] = v[1]

            loop(0, RADIX, one)

        loop(0, R // rows, some)

    def stage_out(it, f):
        dst = gr if it == 0 else out

        def some(g):
            at = pl.ds(pl.multiple_of(g * rows, rows), rows)
            y = eight([(work[0, f, t, at, :], work[1, f, t, at, :]) for t in range(RADIX)], -1)
            for f2 in range(RADIX):
                b, u = divmod(f2, U)
                for part in range(2):
                    v = y[f2][part] * (1.0 / RADIX)
                    gs[b, part, u, f, at, :] = v.astype(jnp.bfloat16) if it == 0 else encode(v)

        loop(0, R // rows, some)
        for j in range(1, A):
            g_copy(it, j, f).start()
        for part in range(2):
            for u in range(U):
                dst[part, u, f, :, mine] = gs[a, part, u, f]

    for copy in locals_[2:]:
        copy.wait()
    for j in range(1, A):
        for part in range(2):
            initials_in(part, j).wait_recv()

    def last(h):
        arrive(C - 1, h)
        loop(0, C, lambda chip: across_in(chip, h).wait_recv())
        loop(0, per, lambda i: product(0, h * per + i))

        @pl.when(h > 0)
        def _():
            loop(0, per, lambda i: stage_in(0, (h - 1) * per + i))

    loop(0, chunks, last)
    loop(0, per, lambda i: stage_in(0, (chunks - 1) * per + i))
    stage_time(0)
    loop(0, RADIX, lambda f: stage_out(0, f))

    def h_sent(f):
        for j in range(1, A):
            h_copy(j, f).wait_send()

    loop(0, RADIX, h_sent)

    def again(f):
        for j in range(1, A):
            g_copy_in(0, j, f).wait_recv()
        product(1, f)

        @pl.when(f > 0)
        def _():
            stage_in(1, f - 1)

    loop(0, RADIX, again)
    by_af[a] = squares[...]

    def af_copy(j):
        return remote(squares, by_af.at[a], m_send.at[j], m_recv.at[j], (ahead(j), s))

    def af_copy_in(j):
        return remote(squares, by_af.at[behind(j)], m_send.at[j], m_recv.at[j], (ahead(j), s))

    for j in range(1, A):
        af_copy(j).start()
    stage_in(1, RADIX - 1)
    stage_time(1)
    for j in range(1, A):
        g_sent = lambda f: g_copy(0, j, f).wait_send()
        loop(0, RADIX, g_sent)
    loop(0, RADIX, lambda f: stage_out(1, f))

    for j in range(1, A):
        af_copy_in(j).wait_recv()
    total = by_af[0]
    for b in range(1, A):
        total = total + by_af[b]
    by_sa[s] = total
    for j in range(1, A):
        af_copy(j).wait_send()
    squares[...] = total

    def sa_copy(j):
        return remote(
            squares, by_sa.at[s], m_send.at[A + j], m_recv.at[A + j], (a, lax.rem(s + j, S))
        )

    def sa_copy_in(j):
        return remote(
            squares, by_sa.at[lax.rem(s + S - j, S)], m_send.at[A + j], m_recv.at[A + j], (a, lax.rem(s + j, S))
        )

    loop(1, S, lambda j: sa_copy(j).start())

    def sent(h):
        @pl.when(c + 1 < C)
        def _():
            loop(0, c + 1, lambda chip: up(chip, h).wait_send())

        @pl.when(c > 0)
        def _():
            loop(c, C, lambda chip: down(chip, h).wait_send())

        loop(0, C, lambda chip: across(chip, h).wait_send())

    loop(0, chunks, sent)
    for j in range(1, A):
        for part in range(2):
            initials(part, j).wait_send()
    loop(0, RADIX, h_sent)
    loop(1, S, lambda j: sa_copy_in(j).wait_recv())
    full = by_sa[0]
    for b in range(1, S):
        full = full + by_sa[b]
    mis[...] = full
    loop(1, S, lambda j: sa_copy(j).wait_send())

    def finish(f):
        for j in range(1, A):
            g_copy_in(1, j, f).wait_recv()
            g_copy(1, j, f).wait_send()

    loop(0, RADIX, finish)


def on_device(counts, data_real, data_imaginary, wave_real, wave_imaginary, primaries_real, primaries_imaginary):
    A, S = counts
    C = S // 2
    L, R, N = data_real.shape
    W = N // A
    U = L // RADIX
    chunks = RADIX if C <= 8 else 1
    turns = 2 * np.pi * np.arange(RADIX * RADIX) / (RADIX * RADIX)
    twiddle = jnp.asarray(np.stack([np.cos(turns), np.sin(turns)]), jnp.float32)
    smem = pl.BlockSpec(memory_space=pltpu.SMEM)
    hbm = pl.BlockSpec(memory_space=pl.ANY)
    vmem = pl.BlockSpec(memory_space=pltpu.VMEM)
    f32, bf16 = jnp.float32, jnp.bfloat16
    dma = pltpu.SemaphoreType.DMA
    split = lambda v: v.reshape(U, RADIX, R, N)
    coded, misfit = pl.pallas_call(
        functools.partial(kernel, A, S, chunks),
        in_specs=[smem, smem, smem, hbm, hbm, hbm, hbm],
        out_specs=[vmem, vmem],
        out_shape=[
            jax.ShapeDtypeStruct((2, U, RADIX, R, N), bf16),
            jax.ShapeDtypeStruct((ITERS, 8, 128), f32),
        ],
        scratch_shapes=[
            pltpu.VMEM((U, RADIX, 2, S, R, N), bf16),
            pltpu.VMEM((2, U, RADIX, R, N), f32),
            pltpu.VMEM((2, A, U, RADIX, R, W), f32),
            pltpu.VMEM((2, RADIX, RADIX, R, W), f32),
            pltpu.VMEM((2, RADIX, RADIX, R, W), f32),
            pltpu.VMEM((A, 2, U, RADIX, R, W), bf16),
            pltpu.VMEM((A, 2, U, RADIX, R, W), bf16),
            pltpu.VMEM((A, 2, U, RADIX, R, W), bf16),
            pltpu.VMEM((2, U, RADIX, R, N), bf16),
            pltpu.VMEM((ITERS, 8, 128), f32),
            pltpu.VMEM((A, ITERS, 8, 128), f32),
            pltpu.VMEM((S, ITERS, 8, 128), f32),
            dma((6,)),
            dma((C, chunks)),
            dma((C, chunks)),
            dma((C, chunks)),
            dma((C, chunks)),
            dma((C, chunks)),
            dma((2, A)),
            dma((2, A)),
            dma((A, RADIX)),
            dma((A, RADIX)),
            dma((ITERS, A, RADIX)),
            dma((ITERS, A, RADIX)),
            dma((A + S,)),
            dma((A + S,)),
        ],
        compiler_params=pltpu.CompilerParams(
            collective_id=0, has_side_effects=True, vmem_limit_bytes=63 * 2**20
        ),
    )(
        wave_real, wave_imaginary, twiddle,
        split(data_real), split(data_imaginary), split(primaries_real), split(primaries_imaginary),
    )
    updated = [decode(coded[part]).reshape(L, R, N) for part in range(2)]
    return (updated[0], updated[1], jnp.sum(misfit, axis=(1, 2)) / (L * A * N * N))


def solution(mesh):
    split = P("af", "sa", None)
    counts = (mesh.shape["af"], mesh.shape["sa"])
    return jax.shard_map(
        functools.partial(on_device, counts),
        mesh=mesh,
        in_specs=(split, split, P("af"), P("af"), split, split),
        out_specs=(split, split, P()),
        check_vma=False,
    )
```

time: 359 us -> 244 us (0.68)
  waiting for transfers between devices: 171 us -> 0 us
  Pallas kernels: 81.9 us -> 234 us
  other arithmetic: 37.9 us -> 8.66 us
  blocking collectives: 28.4 us -> 0 us
  starting transfers between devices: 18.8 us -> 0 us
  between operations: 17.5 us -> 0.66 us
    pallas_call x8 -> x1, Pallas kernels: 81.9 us -> 234 us  [on_device(): pl.pallas_call(functools.partial(kernel, A, S, chunks), in_specs=[smem, s...]
    all_gather x2 -> x0, waiting for transfers between devices: 149 us -> none  [on_device(): wholes.append(lax.all_gather(both, 'sa', axis=0))]
    all_to_all x1 -> x0, blocking collectives: 28.4 us -> none  [exchange(): return lax.all_to_all(values, 'af', split_axis=0, concat_axis=0, tiled=True)]
    convert_element_type x12 -> x0, other arithmetic: 27.4 us -> none  [the longest x4 11.5 us: on_device(): (stepped * (1.0 / z_scale)).astype(WIRE)]
    all_to_all x5 -> x0, waiting for transfers between devices: 21.9 us -> none  [exchange(): return lax.all_to_all(values, 'af', split_axis=0, concat_axis=0, tiled=True)]
    all_to_all x5 -> x0, starting transfers between devices: 18.8 us -> none  [exchange(): return lax.all_to_all(values, 'af', split_axis=0, concat_axis=0, tiled=True)]
  transfers between devices with their start and end apart: 7 -> 0, of which waited for: 4 -> 0; matrix products, arithmetic and copies ran while one was open for 5% -> 0% of each run, Pallas kernels for 15% -> 0%
where the time goes in v1:
time: 244 us
  Pallas kernels  234 us (96%)
  other arithmetic  8.66 us (4%)
    pallas_call x1, Pallas kernels, on_device(): pl.pallas_call(functools.partial(kernel, A, S, chunks), in_specs=[smem, s...  234 us

profile of v1, /device:TPU:0, one launch (start us, length us, event | category | flops | bytes accessed | tf_op | source)
XLA Modules:
  0.0 243.7 jit_solution(12712826718826368659)
XLA Ops:
  0.6 234.3 %shard_map.94 = (bf16[2,2,8,64,512]{4,3,2,1,0:T(8,128)(2,1)}, f32[2,8,128]{2,1,0:T(8,128)}) custom-call(f32[16]{0:T(128)} %wr.1, f32[16]{0:T(128)} %wi.1, f32[2,64]{1,0:T(2,128)} %constant.12.clone.twiddle, bf16[2,8,64,512]{3,2,1,0:T(8,128)(2,1)} %bitcast.28, bf16[2,8,64,512]{3,2,1,0:T(8,128)(2,1)} %bitcast.29, f32[2,8,64,512]{3,2,1,0:T(8,128)} %bitcast.26, ...), custom_call_target="tpu_custom_call" | custom-call | tf_op jit(solution)/shard_map/pallas_call | solution.py:456
  235.0 0.8 reduce_sum.9
  235.8 0.5 broadcast_multiply_fusion
  236.3 0.0 copy-start
  236.3 3.0 %convert_compare_fusion.1 = (pred[1,2,8,64,512]{4,3,2,1,0:T(8,128)(4,1)S(1)}, pred[1,2,8,64,512]{4,3,2,1,0:T(8,128)(4,1)S(1)}, pred[1,2,8,64,512]{4,3,2,1,0:T(8,128)(4,1)S(1)}, pred[1,2,8,64,512]{4,3,2,1,0:T(8,128)(4,1)S(1)}) fusion(bf16[2,2,8,64,512]{4,3,2,1,0:T(8,128)(2,1)} %get-tuple-element.5), kind=kLoop, calls=%fused_computation.2 | loop fusion | flops 3145728 | bytes 4194304 | tf_op jit(solution)/shard_map/gt | solution.py:30
  239.3 0.0 copy-done
  239.3 1.1 fusion.7
  240.4 3.2 %bitcast_select_fusion = (f32[16,64,512]{2,1,0:T(8,128)}, f32[16,64,512]{2,1,0:T(8,128)}) fusion(f32[1,2,8,64,512]{4,3,2,1,0:T(8,128)S(1)} %get-tuple-element.11, pred[1,2,8,64,512]{4,3,2,1,0:T(8,128)(4,1)S(1)} %get-tuple-element.9, pred[1,2,8,64,512]{4,3,2,1,0:T(8,128)(4,1)S(1)} %get-tuple-element.7, pred[1,2,8,64,512]{4,3,2,1,0:T(8,128)(4,1)S(1)} %get-tuple-element.8, ...), kind=kLoop, calls=%fused_computation.14 | loop fusion | flops 3145728 | bytes 10485760 | tf_op jit(solution)/shard_map/jit(_where)/select_n | solution.py:30
Async XLA Ops:
  236.3 3.0 %copy-start = (bf16[2,2,8,64,512]{4,3,2,1,0:T(8,128)(2,1)S(1)}, bf16[2,2,8,64,512]{4,3,2,1,0:T(8,128)(2,1)}, u32[]{:S(2)}) copy-start(bf16[2,2,8,64,512]{4,3,2,1,0:T(8,128)(2,1)} %get-tuple-element.5) | copy-start | bytes 6291460

commit v2 on v1

--- a/solution.py
+++ b/solution.py
@@ -13,6 +13,7 @@
 STEP_LENGTH = 0.02
 THRESHOLD = 0.25
 RADIX = 8
+LENT = 4
 HALF = math.sqrt(0.5)
 REACH = 64.0
 TINY = 2.0**-126
@@ -73,10 +74,11 @@
 
 
 def kernel(
-    A, S, chunks, wr, wi, twiddle, data_r, data_i, prim_r, prim_i, out, mis,
-    whole, current, initial, work, traces, hs, hr, gs, gr, squares, by_af, by_sa,
+    A, S, chunks, lent, wr, wi, twiddle, data_r, data_i, prim_r, prim_i, out, mis,
+    whole, current, initial, work, traces, hs, hr, gs, gr, squares, by_af, by_sa, lent_p, lent_g, lent_h,
     local_sem, up_sem, down_sem, ring_sem, pair_send, pair_recv,
     init_send, init_recv, h_send, h_recv, g_send, g_recv, m_send, m_recv,
+    lp_send, lp_recv, lg_send, lg_recv, lh_send, lh_recv,
 ):
     C = S // 2
     U, _, R, N = data_r.shape
@@ -88,6 +90,25 @@
     c = s // 2
     k = s % 2
     partner = c * 2 + 1 - k
+    kept = chunks - lent
+    F0 = kept * per
+    Q = RADIX - F0
+    if lent:
+        is_end = (c == 0) | (c == C - 1)
+        is_helper = (c == 1) | (c == C - 2)
+        other = jnp.where((c == 0) | (c == C - 2), s + 2, s - 2)
+
+    def goes_up(h):
+        go = c + 1 < C
+        return go & ((h < kept) | (c + 2 < C)) if lent else go
+
+    def goes_down(h):
+        go = c > 0
+        return go & ((h < kept) | (c > 1)) if lent else go
+
+    def keeps(h):
+        return (h < kept) | jnp.logical_not(is_end) if lent else h >= 0
+
     mine = pl.ds(pl.multiple_of(a * W, W), W)
 
     def cols(b):
@@ -162,17 +183,42 @@
     locals_[1].wait()
 
     def first(h):
-        @pl.when(c + 1 < C)
+        @pl.when(goes_up(h))
         def _():
             up(c, h).start()
 
-        @pl.when(c > 0)
+        @pl.when(goes_down(h))
         def _():
             down(c, h).start()
 
-        across(c, h).start()
+        @pl.when(keeps(h))
+        def _():
+            across(c, h).start()
 
     loop(0, chunks, first)
+
+    def lend_p(part, n):
+        src = (prim_r, prim_i)[part]
+        return remote(
+            src.at[:, F0 + n], lent_p.at[part, :, n], lp_send.at[part, n], lp_recv.at[part, n], (a, other)
+        )
+
+    def lend_g(n):
+        return remote(gr.at[:, :, F0 + n], lent_g.at[:, :, n], lg_send.at[n], lg_recv.at[n], (a, other))
+
+    def lend_h(n):
+        return remote(lent_h.at[:, :, :, n], hs.at[:, :, :, F0 + n], lh_send.at[n], lh_recv.at[n], (a, other))
+
+    if lent:
+
+        @pl.when(is_end)
+        def _():
+            def lend(n):
+                lend_p(0, n).start()
+                lend_p(1, n).start()
+
+            loop(0, Q, lend)
+
     for j in range(1, A):
         for part in range(2):
             initials(part, j).start()
@@ -184,7 +230,7 @@
             up(src, h).wait_recv()
             across(src, h).start()
 
-            @pl.when(c + 1 < C)
+            @pl.when(goes_up(h))
             def _():
                 up(src, h).start()
 
@@ -194,11 +240,18 @@
             down(src, h).wait_recv()
             across(src, h).start()
 
-            @pl.when(c > 0)
+            @pl.when(goes_down(h))
             def _():
                 down(src, h).start()
 
-    loop(1, C - 1, lambda d: loop(0, chunks, lambda h: arrive(d, h)))
+    far = jnp.maximum(c, C - 1 - c)
+
+    def pass_on(h, d):
+        @pl.when(keeps(h))
+        def _():
+            arrive(d, h)
+
+    loop(1, far, lambda d: loop(0, chunks, lambda h: pass_on(h, d)))
 
     def h_copy(j, f):
         to = ahead(j)
@@ -226,46 +279,81 @@
             g_send.at[it, j, f], g_recv.at[it, j, f], (ahead(j), s),
         )
 
+    def step_of(it, f, u, at, re, im):
+        qr = wr[u * RADIX + f]
+        qi = wi[u * RADIX + f]
+        whole_r = whole[u, f, 0].reshape(N, N)
+        whole_i = whole[u, f, 1].reshape(N, N)
+        left = jnp.concatenate([re.astype(jnp.bfloat16), im.astype(jnp.bfloat16)], axis=0)
+        pr = jnp.dot(left, whole_r, preferred_element_type=jnp.float32)
+        pi = jnp.dot(left, whole_i, preferred_element_type=jnp.float32)
+        er = whole[u, f, 0, at].astype(jnp.float32) + (pr[:R] - pi[R:]) - (qr * re - qi * im)
+        ei = whole[u, f, 1, at].astype(jnp.float32) + (pi[:R] + pr[R:]) - (qr * im + qi * re)
+        sq = er * er + ei * ei
+        part = sq[:8]
+        for i in range(1, R // 8):
+            part = part + sq[i * 8 : (i + 1) * 8]
+        row = part[:, :128]
+        for i in range(1, N // 128):
+            row = row + part[:, i * 128 : (i + 1) * 128]
+        squares[it] += row
+        eb = jnp.concatenate([er.astype(jnp.bfloat16), ei.astype(jnp.bfloat16)], axis=0)
+        dims = (((1,), (1,)), ((), ()))
+        br = lax.dot_general(eb, whole_r, dims, preferred_element_type=jnp.float32)
+        bi = lax.dot_general(eb, whole_i, dims, preferred_element_type=jnp.float32)
+        dr = encode(STEP_LENGTH * (qr * er + qi * ei - (br[:R] + bi[R:])))
+        di = encode(STEP_LENGTH * (qr * ei - qi * er - (br[R:] - bi[:R])))
+        return dr, di
+
+    def publish(f):
+        for u in range(U):
+            hr[a, 0, u, f] = hs[a, 0, u, f]
+            hr[a, 1, u, f] = hs[a, 1, u, f]
+        for j in range(1, A):
+            h_copy(j, f).start()
+
     def product(it, f):
         def one(u):
-            qr = wr[u * RADIX + f]
-            qi = wi[u * RADIX + f]
             if it == 0:
                 re = current[0, u, f]
                 im = current[1, u, f]
             else:
                 re = gr[0, u, f].astype(jnp.float32)
                 im = gr[1, u, f].astype(jnp.float32)
-            whole_r = whole[u, f, 0].reshape(N, N)
-            whole_i = whole[u, f, 1].reshape(N, N)
-            left = jnp.concatenate([re.astype(jnp.bfloat16), im.astype(jnp.bfloat16)], axis=0)
-            pr = jnp.dot(left, whole_r, preferred_element_type=jnp.float32)
-            pi = jnp.dot(left, whole_i, preferred_element_type=jnp.float32)
-            er = whole[u, f, 0, s].astype(jnp.float32) + (pr[:R] - pi[R:]) - (qr * re - qi * im)
-            ei = whole[u, f, 1, s].astype(jnp.float32) + (pi[:R] + pr[R:]) - (qr * im + qi * re)
-            sq = er * er + ei * ei
-            part = sq[:8]
-            for i in range(1, R // 8):
-                part = part + sq[i * 8 : (i + 1) * 8]
-            row = part[:, :128]
-            for i in range(1, N // 128):
-                row = row + part[:, i * 128 : (i + 1) * 128]
-            squares[it] += row
-            eb = jnp.concatenate([er.astype(jnp.bfloat16), ei.astype(jnp.bfloat16)], axis=0)
-            dims = (((1,), (1,)), ((), ()))
-            br = lax.dot_general(eb, whole_r, dims, preferred_element_type=jnp.float32)
-            bi = lax.dot_general(eb, whole_i, dims, preferred_element_type=jnp.float32)
-            dr = encode(STEP_LENGTH * (qr * er + qi * ei - (br[:R] + bi[R:])))
-            di = encode(STEP_LENGTH * (qr * ei - qi * er - (br[R:] - bi[:R])))
+            dr, di = step_of(it, f, u, s, re, im)
             for b in range(A):
                 hs[b, 0, u, f] = dr[:, b * W : (b + 1) * W]
                 hs[b, 1, u, f] = di[:, b * W : (b + 1) * W]
-            hr[a, 0, u, f] = hs[a, 0, u, f]
-            hr[a, 1, u, f] = hs[a, 1, u, f]
 
         loop(0, U, one)
-        for j in range(1, A):
-            h_copy(j, f).start()
+        publish(f)
+
+    def lent_product(it, n):
+        if it == 0:
+            lend_p(0, n).wait_recv()
+            lend_p(1, n).wait_recv()
+        else:
+            lend_g(n).wait_recv()
+            lend_h(n).wait_send()
+
+        def one(u):
+            if it == 0:
+                re = lent_p[0, u, n]
+                im = lent_p[1, u, n]
+            else:
+                re = lent_g[0, u, n].astype(jnp.float32)
+                im = lent_g[1, u, n].astype(jnp.float32)
+            dr, di = step_of(it, F0 + n, u, other, re, im)
+            for b in range(A):
+                lent_h[b, 0, u, n] = dr[:, b * W : (b + 1) * W]
+                lent_h[b, 1, u, n] = di[:, b * W : (b + 1) * W]
+
+        loop(0, U, one)
+        lend_h(n).start()
+
+    def returned(n):
+        lend_h(n).wait_recv()
+        publish(F0 + n)
 
     def stage_in(it, f):
         for j in range(1, A):
@@ -339,9 +427,24 @@
             initials_in(part, j).wait_recv()
 
     def last(h):
-        arrive(C - 1, h)
-        loop(0, C, lambda chip: across_in(chip, h).wait_recv())
-        loop(0, per, lambda i: product(0, h * per + i))
+        @pl.when(keeps(h))
+        def _():
+            arrive(far, h)
+            loop(0, C, lambda chip: across_in(chip, h).wait_recv())
+
+        if lent:
+
+            @pl.when(is_helper & (h >= kept))
+            def _():
+                loop(0, per, lambda i: lent_product(0, (h - kept) * per + i))
+
+            @pl.when(is_end & (h >= kept))
+            def _():
+                loop(0, per, lambda i: returned((h - kept) * per + i))
+
+        @pl.when(keeps(h))
+        def _():
+            loop(0, per, lambda i: product(0, h * per + i))
 
         @pl.when(h > 0)
         def _():
@@ -350,7 +453,8 @@
     loop(0, chunks, last)
     loop(0, per, lambda i: stage_in(0, (chunks - 1) * per + i))
     stage_time(0)
-    loop(0, RADIX, lambda f: stage_out(0, f))
+    order = lambda i: lax.rem(F0 + i, RADIX)
+    loop(0, RADIX, lambda i: stage_out(0, order(i)))
 
     def h_sent(f):
         for j in range(1, A):
@@ -358,16 +462,53 @@
 
     loop(0, RADIX, h_sent)
 
-    def again(f):
+    def lends(f):
+        return is_end & (f >= F0)
+
+    def again(i):
+        f = order(i)
         for j in range(1, A):
             g_copy_in(0, j, f).wait_recv()
-        product(1, f)
-
-        @pl.when(f > 0)
-        def _():
-            stage_in(1, f - 1)
+        if lent:
+
+            @pl.when(lends(f))
+            def _():
+                lend_g(f - F0).start()
+
+            @pl.when(jnp.logical_not(lends(f)))
+            def _():
+                product(1, f)
+
+            @pl.when(is_helper & (i >= 2) & (lax.rem(i, 2) == 0) & (i < 2 * Q + 2))
+            def _():
+                lent_product(1, i // 2 - 1)
+
+            before = order(i + RADIX - 1)
+
+            @pl.when((i > 0) & jnp.logical_not(lends(before)))
+            def _():
+                stage_in(1, before)
+
+        else:
+            product(1, f)
+
+            @pl.when(i > 0)
+            def _():
+                stage_in(1, order(i + RADIX - 1))
 
     loop(0, RADIX, again)
+    if lent:
+        late = (RADIX - 1) // 2
+
+        @pl.when(is_helper)
+        def _():
+            if late < Q:
+                loop(late, Q, lambda n: lent_product(1, n))
+
+        @pl.when(is_end)
+        def _():
+            loop(0, Q, returned)
+
     by_af[a] = squares[...]
 
     def af_copy(j):
@@ -378,7 +519,13 @@
 
     for j in range(1, A):
         af_copy(j).start()
-    stage_in(1, RADIX - 1)
+    stage_in(1, order(RADIX - 1))
+    if lent:
+
+        @pl.when(is_end)
+        def _():
+            loop(0, Q, lambda n: stage_in(1, F0 + n))
+
     stage_time(1)
     for j in range(1, A):
         g_sent = lambda f: g_copy(0, j, f).wait_send()
@@ -408,17 +555,34 @@
     loop(1, S, lambda j: sa_copy(j).start())
 
     def sent(h):
-        @pl.when(c + 1 < C)
+        @pl.when(goes_up(h))
         def _():
             loop(0, c + 1, lambda chip: up(chip, h).wait_send())
 
-        @pl.when(c > 0)
+        @pl.when(goes_down(h))
         def _():
             loop(c, C, lambda chip: down(chip, h).wait_send())
 
-        loop(0, C, lambda chip: across(chip, h).wait_send())
+        @pl.when(keeps(h))
+        def _():
+            loop(0, C, lambda chip: across(chip, h).wait_send())
 
     loop(0, chunks, sent)
+    if lent:
+
+        @pl.when(is_end)
+        def _():
+            def lent_out(n):
+                lend_p(0, n).wait_send()
+                lend_p(1, n).wait_send()
+                lend_g(n).wait_send()
+
+            loop(0, Q, lent_out)
+
+        @pl.when(is_helper)
+        def _():
+            loop(0, Q, lambda n: lend_h(n).wait_send())
+
     for j in range(1, A):
         for part in range(2):
             initials(part, j).wait_send()
@@ -445,6 +609,8 @@
     W = N // A
     U = L // RADIX
     chunks = RADIX if C <= 8 else 1
+    lent = LENT if C >= 4 and chunks > LENT else 0
+    Q = max(1, lent * RADIX // chunks)
     turns = 2 * np.pi * np.arange(RADIX * RADIX) / (RADIX * RADIX)
     twiddle = jnp.asarray(np.stack([np.cos(turns), np.sin(turns)]), jnp.float32)
     smem = pl.BlockSpec(memory_space=pltpu.SMEM)
@@ -454,7 +620,7 @@
     dma = pltpu.SemaphoreType.DMA
     split = lambda v: v.reshape(U, RADIX, R, N)
     coded, misfit = pl.pallas_call(
-        functools.partial(kernel, A, S, chunks),
+        functools.partial(kernel, A, S, chunks, lent),
         in_specs=[smem, smem, smem, hbm, hbm, hbm, hbm],
         out_specs=[vmem, vmem],
         out_shape=[
@@ -474,6 +640,9 @@
             pltpu.VMEM((ITERS, 8, 128), f32),
             pltpu.VMEM((A, ITERS, 8, 128), f32),
             pltpu.VMEM((S, ITERS, 8, 128), f32),
+            pltpu.VMEM((2, U, Q, R, N), f32),
+            pltpu.VMEM((2, U, Q, R, N), bf16),
+            pltpu.VMEM((A, 2, U, Q, R, W), bf16),
             dma((6,)),
             dma((C, chunks)),
             dma((C, chunks)),
@@ -488,6 +657,12 @@
             dma((ITERS, A, RADIX)),
             dma((A + S,)),
             dma((A + S,)),
+            dma((2, Q)),
+            dma((2, Q)),
+            dma((Q,)),
+            dma((Q,)),
+            dma((Q,)),
+            dma((Q,)),
         ],
         compiler_params=pltpu.CompilerParams(
             collective_id=0, has_side_effects=True, vmem_limit_bytes=63 * 2**20

time: 244 us -> 211 us (0.86)
  Pallas kernels: 234 us -> 201 us
    pallas_call x1, Pallas kernels: 234 us -> 201 us  [on_device(): pl.pallas_call(functools.partial(kernel, A, S, chunks, lent), in_specs=[s...]
where the time goes in v2:
time: 211 us; the launch traced here: 210 us
  Pallas kernels  201 us (95%)
  other arithmetic  8.66 us (4%)
    pallas_call x1, Pallas kernels, on_device(): pl.pallas_call(functools.partial(kernel, A, S, chunks, lent), in_specs=[s...  201 us

profile of v2, /device:TPU:0, one launch (start us, length us, event | category | flops | bytes accessed | tf_op | source)
XLA Modules:
  0.0 210.4 jit_solution(4208252549600582997)
XLA Ops:
  0.6 201.1 %shard_map.94 = (bf16[2,2,8,64,512]{4,3,2,1,0:T(8,128)(2,1)}, f32[2,8,128]{2,1,0:T(8,128)}) custom-call(f32[16]{0:T(128)} %wr.1, f32[16]{0:T(128)} %wi.1, f32[2,64]{1,0:T(2,128)} %constant.12.clone.twiddle, bf16[2,8,64,512]{3,2,1,0:T(8,128)(2,1)} %bitcast.28, bf16[2,8,64,512]{3,2,1,0:T(8,128)(2,1)} %bitcast.29, f32[2,8,64,512]{3,2,1,0:T(8,128)} %bitcast.26, ...), custom_call_target="tpu_custom_call" | custom-call | tf_op jit(solution)/shard_map/pallas_call | solution.py:622
  201.7 0.8 reduce_sum.9
  202.5 0.5 broadcast_multiply_fusion
  203.0 0.0 copy-start
  203.0 3.0 %convert_compare_fusion.1 = (pred[1,2,8,64,512]{4,3,2,1,0:T(8,128)(4,1)S(1)}, pred[1,2,8,64,512]{4,3,2,1,0:T(8,128)(4,1)S(1)}, pred[1,2,8,64,512]{4,3,2,1,0:T(8,128)(4,1)S(1)}, pred[1,2,8,64,512]{4,3,2,1,0:T(8,128)(4,1)S(1)}) fusion(bf16[2,2,8,64,512]{4,3,2,1,0:T(8,128)(2,1)} %get-tuple-element.5), kind=kLoop, calls=%fused_computation.2 | loop fusion | flops 3145728 | bytes 4194304 | tf_op jit(solution)/shard_map/gt | solution.py:31
  206.1 0.0 copy-done
  206.1 1.1 fusion.7
  207.2 3.2 %bitcast_select_fusion = (f32[16,64,512]{2,1,0:T(8,128)}, f32[16,64,512]{2,1,0:T(8,128)}) fusion(f32[1,2,8,64,512]{4,3,2,1,0:T(8,128)S(1)} %get-tuple-element.11, pred[1,2,8,64,512]{4,3,2,1,0:T(8,128)(4,1)S(1)} %get-tuple-element.9, pred[1,2,8,64,512]{4,3,2,1,0:T(8,128)(4,1)S(1)} %get-tuple-element.7, pred[1,2,8,64,512]{4,3,2,1,0:T(8,128)(4,1)S(1)} %get-tuple-element.8, ...), kind=kLoop, calls=%fused_computation.14 | loop fusion | flops 3145728 | bytes 10485760 | tf_op jit(solution)/shard_map/jit(_where)/select_n | solution.py:31
Async XLA Ops:
  203.0 3.0 %copy-start = (bf16[2,2,8,64,512]{4,3,2,1,0:T(8,128)(2,1)S(1)}, bf16[2,2,8,64,512]{4,3,2,1,0:T(8,128)(2,1)}, u32[]{:S(2)}) copy-start(bf16[2,2,8,64,512]{4,3,2,1,0:T(8,128)(2,1)} %get-tuple-element.5) | copy-start | bytes 6291460

commit v3 on v2

--- a/solution.py
+++ b/solution.py
@@ -13,7 +13,7 @@
 STEP_LENGTH = 0.02
 THRESHOLD = 0.25
 RADIX = 8
-LENT = 4
+LENT = 3
 HALF = math.sqrt(0.5)
 REACH = 64.0
 TINY = 2.0**-126
@@ -27,8 +27,8 @@
 
 def decode(code):
     v = code.astype(jnp.float32)
-    r = lax.rsqrt(lax.rsqrt(jnp.maximum(jnp.abs(v), TINY))) * REACH
-    return jnp.where(v > 0, r, jnp.where(v < 0, -r, 0.0))
+    y = lax.rsqrt(jnp.maximum(jnp.abs(v), TINY))
+    return ((v * y) * y) * (lax.rsqrt(y) * REACH)
 
 
 def add(a, b):
@@ -75,10 +75,10 @@
 
 def kernel(
     A, S, chunks, lent, wr, wi, twiddle, data_r, data_i, prim_r, prim_i, out, mis,
-    whole, current, initial, work, traces, hs, hr, gs, gr, squares, by_af, by_sa, lent_p, lent_g, lent_h,
+    whole, current, initial, work, traces, hs, hr, gs, gr, squares, by_af, by_sa, lent_g, lent_h,
     local_sem, up_sem, down_sem, ring_sem, pair_send, pair_recv,
     init_send, init_recv, h_send, h_recv, g_send, g_recv, m_send, m_recv,
-    lp_send, lp_recv, lg_send, lg_recv, lh_send, lh_recv,
+    lg_send, lg_recv, lh_send, lh_recv, out_sem,
 ):
     C = S // 2
     U, _, R, N = data_r.shape
@@ -136,8 +136,6 @@
         pltpu.make_async_copy(prim_r.at[:, :, :, mine], initial.at[0, a], local_sem.at[4]),
         pltpu.make_async_copy(prim_i.at[:, :, :, mine], initial.at[1, a], local_sem.at[5]),
     ]
-    for copy in locals_:
-        copy.start()
     squares[...] = jnp.zeros_like(squares)
     pl.semaphore_wait(barrier, A - 1 + S - 1)
 
@@ -149,6 +147,9 @@
             src_ref=src, dst_ref=dst, send_sem=send, recv_sem=recv, device_id=device, device_id_type=MESH
         )
 
+    def own(part, h):
+        return (data_r, data_i)[part].at[:, pl.ds(h * per, per)]
+
     def up(chip, h):
         ref = shard(chip, k, h)
         return remote(ref, ref, up_sem.at[chip, h], ring_sem.at[chip, h], (a, lax.rem(s + 2, S)))
@@ -161,6 +162,21 @@
         ref = shard(chip, k, h)
         return remote(ref, ref, pair_send.at[chip, h], pair_recv.at[chip, h], (a, partner))
 
+    def own_up(part, h):
+        return remote(
+            own(part, h), shard(c, k, h).at[:, :, part], up_sem.at[c, h], ring_sem.at[c, h], (a, lax.rem(s + 2, S))
+        )
+
+    def own_down(part, h):
+        return remote(
+            own(part, h), shard(c, k, h).at[:, :, part], down_sem.at[c, h], ring_sem.at[c, h], (a, lax.rem(s + S - 2, S))
+        )
+
+    def own_across(part, h):
+        return remote(
+            own(part, h), shard(c, k, h).at[:, :, part], pair_send.at[c, h], pair_recv.at[c, h], (a, partner)
+        )
+
     def across_in(chip, h):
         ref = shard(chip, 1 - k, h)
         return remote(ref, ref, pair_send.at[chip, h], pair_recv.at[chip, h], (a, partner))
@@ -179,29 +195,23 @@
             init_send.at[part, j], init_recv.at[part, j], (ahead(j), s),
         )
 
-    locals_[0].wait()
-    locals_[1].wait()
-
     def first(h):
         @pl.when(goes_up(h))
         def _():
-            up(c, h).start()
+            own_up(0, h).start()
+            own_up(1, h).start()
 
         @pl.when(goes_down(h))
         def _():
-            down(c, h).start()
+            own_down(0, h).start()
+            own_down(1, h).start()
 
         @pl.when(keeps(h))
         def _():
-            across(c, h).start()
+            own_across(0, h).start()
+            own_across(1, h).start()
 
     loop(0, chunks, first)
-
-    def lend_p(part, n):
-        src = (prim_r, prim_i)[part]
-        return remote(
-            src.at[:, F0 + n], lent_p.at[part, :, n], lp_send.at[part, n], lp_recv.at[part, n], (a, other)
-        )
 
     def lend_g(n):
         return remote(gr.at[:, :, F0 + n], lent_g.at[:, :, n], lg_send.at[n], lg_recv.at[n], (a, other))
@@ -209,19 +219,25 @@
     def lend_h(n):
         return remote(lent_h.at[:, :, :, n], hs.at[:, :, :, F0 + n], lh_send.at[n], lh_recv.at[n], (a, other))
 
-    if lent:
-
-        @pl.when(is_end)
-        def _():
-            def lend(n):
-                lend_p(0, n).start()
-                lend_p(1, n).start()
-
-            loop(0, Q, lend)
-
     for j in range(1, A):
         for part in range(2):
             initials(part, j).start()
+    for copy in locals_:
+        copy.start()
+    for copy in locals_[2:4]:
+        copy.wait()
+    if lent:
+
+        @pl.when(is_end)
+        def _():
+            def lend(n):
+                for part in range(2):
+                    for u in range(U):
+                        gr[part, u, F0 + n] = current[part, u, F0 + n].astype(jnp.bfloat16)
+                lend_g(n).start()
+
+            loop(0, Q, lend)
+
 
     def arrive(d, h):
         @pl.when(c >= d)
@@ -329,20 +345,13 @@
         publish(f)
 
     def lent_product(it, n):
-        if it == 0:
-            lend_p(0, n).wait_recv()
-            lend_p(1, n).wait_recv()
-        else:
-            lend_g(n).wait_recv()
+        lend_g(n).wait_recv()
+        if it > 0:
             lend_h(n).wait_send()
 
         def one(u):
-            if it == 0:
-                re = lent_p[0, u, n]
-                im = lent_p[1, u, n]
-            else:
-                re = lent_g[0, u, n].astype(jnp.float32)
-                im = lent_g[1, u, n].astype(jnp.float32)
+            re = lent_g[0, u, n].astype(jnp.float32)
+            im = lent_g[1, u, n].astype(jnp.float32)
             dr, di = step_of(it, F0 + n, u, other, re, im)
             for b in range(A):
                 lent_h[b, 0, u, n] = dr[:, b * W : (b + 1) * W]
@@ -353,6 +362,7 @@
 
     def returned(n):
         lend_h(n).wait_recv()
+        lend_g(n).wait_send()
         publish(F0 + n)
 
     def stage_in(it, f):
@@ -401,9 +411,10 @@
 
         loop(0, R // rows, some)
 
+    def own_out(f):
+        return pltpu.make_async_copy(gs.at[a, :, :, f], out.at[:, :, f, :, mine], out_sem.at[f])
+
     def stage_out(it, f):
-        dst = gr if it == 0 else out
-
         def some(g):
             at = pl.ds(pl.multiple_of(g * rows, rows), rows)
             y = eight([(work[0, f, t, at, :], work[1, f, t, at, :]) for t in range(RADIX)], -1)
@@ -416,11 +427,14 @@
         loop(0, R // rows, some)
         for j in range(1, A):
             g_copy(it, j, f).start()
-        for part in range(2):
-            for u in range(U):
-                dst[part, u, f, :, mine] = gs[a, part, u, f]
-
-    for copy in locals_[2:]:
+        if it == 0:
+            for part in range(2):
+                for u in range(U):
+                    gr[part, u, f, :, mine] = gs[a, part, u, f]
+        else:
+            own_out(f).start()
+
+    for copy in locals_[:2] + locals_[4:]:
         copy.wait()
     for j in range(1, A):
         for part in range(2):
@@ -569,15 +583,6 @@
 
     loop(0, chunks, sent)
     if lent:
-
-        @pl.when(is_end)
-        def _():
-            def lent_out(n):
-                lend_p(0, n).wait_send()
-                lend_p(1, n).wait_send()
-                lend_g(n).wait_send()
-
-            loop(0, Q, lent_out)
 
         @pl.when(is_helper)
         def _():
@@ -591,13 +596,15 @@
     full = by_sa[0]
     for b in range(1, S):
         full = full + by_sa[b]
-    mis[...] = full
+    for it in range(ITERS):
+        mis[it] = jnp.sum(full[it]) * (1.0 / (U * RADIX * A * N * N))
     loop(1, S, lambda j: sa_copy(j).wait_send())
 
     def finish(f):
         for j in range(1, A):
             g_copy_in(1, j, f).wait_recv()
             g_copy(1, j, f).wait_send()
+        own_out(f).wait()
 
     loop(0, RADIX, finish)
 
@@ -615,17 +622,16 @@
     twiddle = jnp.asarray(np.stack([np.cos(turns), np.sin(turns)]), jnp.float32)
     smem = pl.BlockSpec(memory_space=pltpu.SMEM)
     hbm = pl.BlockSpec(memory_space=pl.ANY)
-    vmem = pl.BlockSpec(memory_space=pltpu.VMEM)
     f32, bf16 = jnp.float32, jnp.bfloat16
     dma = pltpu.SemaphoreType.DMA
     split = lambda v: v.reshape(U, RADIX, R, N)
     coded, misfit = pl.pallas_call(
         functools.partial(kernel, A, S, chunks, lent),
         in_specs=[smem, smem, smem, hbm, hbm, hbm, hbm],
-        out_specs=[vmem, vmem],
+        out_specs=[hbm, smem],
         out_shape=[
             jax.ShapeDtypeStruct((2, U, RADIX, R, N), bf16),
-            jax.ShapeDtypeStruct((ITERS, 8, 128), f32),
+            jax.ShapeDtypeStruct((ITERS,), f32),
         ],
         scratch_shapes=[
             pltpu.VMEM((U, RADIX, 2, S, R, N), bf16),
@@ -640,7 +646,6 @@
             pltpu.VMEM((ITERS, 8, 128), f32),
             pltpu.VMEM((A, ITERS, 8, 128), f32),
             pltpu.VMEM((S, ITERS, 8, 128), f32),
-            pltpu.VMEM((2, U, Q, R, N), f32),
             pltpu.VMEM((2, U, Q, R, N), bf16),
             pltpu.VMEM((A, 2, U, Q, R, W), bf16),
             dma((6,)),
@@ -657,12 +662,11 @@
             dma((ITERS, A, RADIX)),
             dma((A + S,)),
             dma((A + S,)),
-            dma((2, Q)),
-            dma((2, Q)),
             dma((Q,)),
             dma((Q,)),
             dma((Q,)),
             dma((Q,)),
+            dma((RADIX,)),
         ],
         compiler_params=pltpu.CompilerParams(
             collective_id=0, has_side_effects=True, vmem_limit_bytes=63 * 2**20
@@ -672,7 +676,7 @@
         split(data_real), split(data_imaginary), split(primaries_real), split(primaries_imaginary),
     )
     updated = [decode(coded[part]).reshape(L, R, N) for part in range(2)]
-    return (updated[0], updated[1], jnp.sum(misfit, axis=(1, 2)) / (L * A * N * N))
+    return (updated[0], updated[1], misfit)
 
 
 def solution(mesh):

time: 211 us -> 201 us (0.953)
  Pallas kernels: 201 us -> 195 us
  other arithmetic: 8.66 us -> 3.37 us
  local copies, waits for them, and re-layouts: 0.01 us -> 2.28 us
    pallas_call x1, Pallas kernels: 201 us -> 195 us  [on_device(): pl.pallas_call(functools.partial(kernel, A, S, chunks, lent), in_specs=[s...]
    select_n x1 -> x0, other arithmetic: 3.23 us -> none  [decode(): return jnp.where(v > 0, r, jnp.where(v < 0, -r, 0.0))]
    gt x1 -> x0, other arithmetic: 3.03 us -> none  [decode(): return jnp.where(v > 0, r, jnp.where(v < 0, -r, 0.0))]
    mul x1, other arithmetic: 1.09 us -> 3.37 us  [decode(): return v * y * y * (lax.rsqrt(y) * REACH)]
where the time goes in v3:
time: 201 us
  Pallas kernels  195 us (97%)
  other arithmetic  3.37 us (2%)
  local copies, waits for them, and re-layouts  2.28 us (1%)
    pallas_call x1, Pallas kernels, on_device(): pl.pallas_call(functools.partial(kernel, A, S, chunks, lent), in_specs=[s...  195 us

profile of v3, /device:TPU:0, one launch (start us, length us, event | category | flops | bytes accessed | tf_op | source)
XLA Modules:
  0.0 200.9 jit_solution(7148187679546770732)
XLA Ops:
  0.6 194.6 %shard_map.94 = (bf16[2,2,8,64,512]{4,3,2,1,0:T(8,128)(2,1)}, f32[2]{0:T(128)}) custom-call(f32[16]{0:T(128)} %wr.1, f32[16]{0:T(128)} %wi.1, f32[2,64]{1,0:T(2,128)} %constant.6.clone.twiddle, bf16[2,8,64,512]{3,2,1,0:T(8,128)(2,1)} %bitcast.12, bf16[2,8,64,512]{3,2,1,0:T(8,128)(2,1)} %bitcast.13, f32[2,8,64,512]{3,2,1,0:T(8,128)} %bitcast.10, ...), custom_call_target="tpu_custom_call" | custom-call | tf_op jit(solution)/shard_map/pallas_call | solution.py:628
  195.2 1.8 fusion.10
  197.0 0.0 copy-start
  197.0 3.4 %fusion.4 = (f32[16,64,512]{2,1,0:T(8,128)}, f32[16,64,512]{2,1,0:T(8,128)}) fusion(bf16[1,2,8,64,512]{4,3,2,1,0:T(8,128)(2,1)S(1)} %get-tuple-element.8, bf16[1,2,8,64,512]{4,3,2,1,0:T(8,128)(2,1)S(1)} %get-tuple-element.7), kind=kLoop, calls=%fused_computation.8 | loop fusion | flops 7340032 | bytes 6291456 | tf_op jit(solution)/shard_map/mul | solution.py:31
  200.4 0.0 copy-done
  200.4 0.5 copy.11
Async XLA Ops:
  197.0 3.4 %copy-start = (f32[2]{0:T(128)S(1)}, f32[2]{0:T(128)}, u32[]{:S(2)}) copy-start(f32[2]{0:T(128)} %get-tuple-element.16) | copy-start | bytes 28

commit v4 on v3

--- a/solution.py
+++ b/solution.py
@@ -14,6 +14,7 @@
 THRESHOLD = 0.25
 RADIX = 8
 LENT = 3
+LAG = 4
 HALF = math.sqrt(0.5)
 REACH = 64.0
 TINY = 2.0**-126
@@ -74,25 +75,28 @@
 
 
 def kernel(
-    A, S, chunks, lent, wr, wi, twiddle, data_r, data_i, prim_r, prim_i, out, mis,
+    A, S, chunks, F0, wr, wi, twiddle, data_r, data_i, prim_r, prim_i, out_r, out_i, mis,
     whole, current, initial, work, traces, hs, hr, gs, gr, squares, by_af, by_sa, lent_g, lent_h,
     local_sem, up_sem, down_sem, ring_sem, pair_send, pair_recv,
-    init_send, init_recv, h_send, h_recv, g_send, g_recv, m_send, m_recv,
+    init_send, init_recv, h_send, h_recv, g_send, g_recv, o_send, o_recv, m_send, m_recv,
     lg_send, lg_recv, lh_send, lh_recv, out_sem,
 ):
     C = S // 2
-    U, _, R, N = data_r.shape
+    L, R, N = prim_r.shape
+    U = L // RADIX
     W = N // A
     per = RADIX // chunks
+    halves = 2 if R % 32 == 0 else 1
+    half = R // halves
     rows = 16 if R % 16 == 0 else 8
     a = lax.axis_index("af")
     s = lax.axis_index("sa")
     c = s // 2
     k = s % 2
     partner = c * 2 + 1 - k
-    kept = chunks - lent
-    F0 = kept * per
-    Q = RADIX - F0
+    kept = F0 // per
+    lent = chunks - kept
+    Q = L - F0 * U
     if lent:
         is_end = (c == 0) | (c == C - 1)
         is_helper = (c == 1) | (c == C - 2)
@@ -110,6 +114,9 @@
         return (h < kept) | jnp.logical_not(is_end) if lent else h >= 0
 
     mine = pl.ds(pl.multiple_of(a * W, W), W)
+
+    def place(n):
+        return lax.rem(n, U) * RADIX + n // U
 
     def cols(b):
         return pl.ds(pl.multiple_of(b * W, W), W)
@@ -133,9 +140,11 @@
         pltpu.make_async_copy(data_i, whole.at[:, :, 1, s], local_sem.at[1]),
         pltpu.make_async_copy(prim_r, current.at[0], local_sem.at[2]),
         pltpu.make_async_copy(prim_i, current.at[1], local_sem.at[3]),
-        pltpu.make_async_copy(prim_r.at[:, :, :, mine], initial.at[0, a], local_sem.at[4]),
-        pltpu.make_async_copy(prim_i.at[:, :, :, mine], initial.at[1, a], local_sem.at[5]),
+        pltpu.make_async_copy(prim_r.at[:, :, mine], initial.at[0, a], local_sem.at[4]),
+        pltpu.make_async_copy(prim_i.at[:, :, mine], initial.at[1, a], local_sem.at[5]),
     ]
+    for copy in locals_:
+        copy.start()
     squares[...] = jnp.zeros_like(squares)
     pl.semaphore_wait(barrier, A - 1 + S - 1)
 
@@ -184,14 +193,14 @@
     def initials(part, j):
         src = (prim_r, prim_i)[part]
         return remote(
-            src.at[:, :, :, cols(ahead(j))], initial.at[part, a],
+            src.at[:, :, cols(ahead(j))], initial.at[part, a],
             init_send.at[part, j], init_recv.at[part, j], (ahead(j), s),
         )
 
     def initials_in(part, j):
         src = (prim_r, prim_i)[part]
         return remote(
-            src.at[:, :, :, mine], initial.at[part, behind(j)],
+            src.at[:, :, mine], initial.at[part, behind(j)],
             init_send.at[part, j], init_recv.at[part, j], (ahead(j), s),
         )
 
@@ -214,16 +223,14 @@
     loop(0, chunks, first)
 
     def lend_g(n):
-        return remote(gr.at[:, :, F0 + n], lent_g.at[:, :, n], lg_send.at[n], lg_recv.at[n], (a, other))
+        return remote(gr.at[:, lax.rem(n, U), F0 + n // U], lent_g.at[:, n], lg_send.at[n], lg_recv.at[n], (a, other))
 
     def lend_h(n):
-        return remote(lent_h.at[:, :, :, n], hs.at[:, :, :, F0 + n], lh_send.at[n], lh_recv.at[n], (a, other))
+        return remote(lent_h.at[:, :, n], hs.at[:, :, lax.rem(n, U), F0 + n // U], lh_send.at[n], lh_recv.at[n], (a, other))
 
     for j in range(1, A):
         for part in range(2):
             initials(part, j).start()
-    for copy in locals_:
-        copy.start()
     for copy in locals_[2:4]:
         copy.wait()
     if lent:
@@ -231,9 +238,9 @@
         @pl.when(is_end)
         def _():
             def lend(n):
+                at = place(F0 * U + n)
                 for part in range(2):
-                    for u in range(U):
-                        gr[part, u, F0 + n] = current[part, u, F0 + n].astype(jnp.bfloat16)
+                    gr[part, lax.rem(n, U), F0 + n // U] = current[part, at].astype(jnp.bfloat16)
                 lend_g(n).start()
 
             loop(0, Q, lend)
@@ -269,35 +276,46 @@
 
     loop(1, far, lambda d: loop(0, chunks, lambda h: pass_on(h, d)))
 
-    def h_copy(j, f):
+    def strip(p):
+        return pl.ds(pl.multiple_of(p * half, half), half)
+
+    def h_copy(j, f, p):
+        to, q, at = ahead(j), f * halves + p, strip(p)
+        return remote(hs.at[to, :, :, f, at], hr.at[a, :, :, f, at], h_send.at[j, q], h_recv.at[j, q], (to, s))
+
+    def h_copy_in(j, f, p):
+        q, at = f * halves + p, strip(p)
+        return remote(
+            hs.at[a, :, :, f, at], hr.at[behind(j), :, :, f, at], h_send.at[j, q], h_recv.at[j, q], (ahead(j), s)
+        )
+
+    def g_copy(j, f):
         to = ahead(j)
-        return remote(
-            hs.at[to, :, :, f], hr.at[a, :, :, f], h_send.at[j, f], h_recv.at[j, f], (to, s)
-        )
-
-    def h_copy_in(j, f):
-        return remote(
-            hs.at[a, :, :, f], hr.at[behind(j), :, :, f], h_send.at[j, f], h_recv.at[j, f], (ahead(j), s)
-        )
-
-    def g_copy(it, j, f):
-        to = ahead(j)
-        dst = gr if it == 0 else out
-        return remote(
-            gs.at[to, :, :, f], dst.at[:, :, f, :, mine],
-            g_send.at[it, j, f], g_recv.at[it, j, f], (to, s),
-        )
-
-    def g_copy_in(it, j, f):
-        dst = gr if it == 0 else out
-        return remote(
-            gs.at[a, :, :, f], dst.at[:, :, f, :, cols(behind(j))],
-            g_send.at[it, j, f], g_recv.at[it, j, f], (ahead(j), s),
-        )
-
-    def step_of(it, f, u, at, re, im):
-        qr = wr[u * RADIX + f]
-        qi = wi[u * RADIX + f]
+        return remote(gs.at[to, :, :, f], gr.at[:, :, f, :, mine], g_send.at[j, f], g_recv.at[j, f], (to, s))
+
+    def g_copy_in(j, f):
+        return remote(
+            gs.at[a, :, :, f], gr.at[:, :, f, :, cols(behind(j))], g_send.at[j, f], g_recv.at[j, f], (ahead(j), s)
+        )
+
+    def o_copy(part, j, m, p):
+        to, q, at, pair = ahead(j), m * halves + p, strip(p), pl.ds(m * 2, 2)
+        return remote(
+            gs.at[to, part, :, pair, at], (out_r, out_i)[part].at[:, pair, at, mine],
+            o_send.at[j, q], o_recv.at[j, q], (to, s),
+        )
+
+    def o_both(j, m, p):
+        q, at, pair = m * halves + p, strip(p), pl.ds(m * 2, 2)
+        return remote(
+            gs.at[a, :, :, pair, at], gr.at[:, :, pair, at, cols(behind(j))],
+            o_send.at[j, q], o_recv.at[j, q], (ahead(j), s),
+        )
+
+    def step_of(it, l, at, re, im):
+        u, f = l // RADIX, lax.rem(l, RADIX)
+        qr = wr[l]
+        qi = wi[l]
         whole_r = whole[u, f, 0].reshape(N, N)
         whole_i = whole[u, f, 1].reshape(N, N)
         left = jnp.concatenate([re.astype(jnp.bfloat16), im.astype(jnp.bfloat16)], axis=0)
@@ -321,64 +339,63 @@
         di = encode(STEP_LENGTH * (qr * ei - qi * er - (br[R:] - bi[:R])))
         return dr, di
 
-    def publish(f):
-        for u in range(U):
-            hr[a, 0, u, f] = hs[a, 0, u, f]
-            hr[a, 1, u, f] = hs[a, 1, u, f]
-        for j in range(1, A):
-            h_copy(j, f).start()
-
-    def product(it, f):
-        def one(u):
-            if it == 0:
-                re = current[0, u, f]
-                im = current[1, u, f]
-            else:
-                re = gr[0, u, f].astype(jnp.float32)
-                im = gr[1, u, f].astype(jnp.float32)
-            dr, di = step_of(it, f, u, s, re, im)
-            for b in range(A):
-                hs[b, 0, u, f] = dr[:, b * W : (b + 1) * W]
-                hs[b, 1, u, f] = di[:, b * W : (b + 1) * W]
-
-        loop(0, U, one)
-        publish(f)
+    def publish(it, l):
+        u, f = l // RADIX, lax.rem(l, RADIX)
+        hr[a, 0, u, f] = hs[a, 0, u, f]
+        hr[a, 1, u, f] = hs[a, 1, u, f]
+
+        @pl.when(u == U - 1)
+        def _():
+            for p in range(halves if it == 0 else 1):
+                for j in range(1, A):
+                    h_copy(j, f, p).start()
+
+    def product(it, l):
+        u, f = l // RADIX, lax.rem(l, RADIX)
+        if it == 0:
+            re, im = current[0, l], current[1, l]
+        else:
+            re, im = gr[0, u, f].astype(jnp.float32), gr[1, u, f].astype(jnp.float32)
+        dr, di = step_of(it, l, s, re, im)
+        for b in range(A):
+            hs[b, 0, u, f] = dr[:, b * W : (b + 1) * W]
+            hs[b, 1, u, f] = di[:, b * W : (b + 1) * W]
+        publish(it, l)
 
     def lent_product(it, n):
         lend_g(n).wait_recv()
         if it > 0:
             lend_h(n).wait_send()
-
-        def one(u):
-            re = lent_g[0, u, n].astype(jnp.float32)
-            im = lent_g[1, u, n].astype(jnp.float32)
-            dr, di = step_of(it, F0 + n, u, other, re, im)
-            for b in range(A):
-                lent_h[b, 0, u, n] = dr[:, b * W : (b + 1) * W]
-                lent_h[b, 1, u, n] = di[:, b * W : (b + 1) * W]
-
-        loop(0, U, one)
+        dr, di = step_of(
+            it, place(F0 * U + n), other, lent_g[0, n].astype(jnp.float32), lent_g[1, n].astype(jnp.float32)
+        )
+        for b in range(A):
+            lent_h[b, 0, n] = dr[:, b * W : (b + 1) * W]
+            lent_h[b, 1, n] = di[:, b * W : (b + 1) * W]
         lend_h(n).start()
 
-    def returned(n):
+    def returned(it, n):
         lend_h(n).wait_recv()
         lend_g(n).wait_send()
-        publish(F0 + n)
-
-    def stage_in(it, f):
+        publish(it, place(F0 * U + n))
+
+    blocks = half // rows
+
+    def stage_in(it, f, p):
         for j in range(1, A):
-            h_copy_in(j, f).wait_recv()
+            h_copy_in(j, f, p).wait_recv()
 
         def some(g):
             at = pl.ds(pl.multiple_of(g * rows, rows), rows)
             x = []
             for f2 in range(RADIX):
                 b, u = divmod(f2, U)
+                l = u * RADIX + f
                 re = decode(hr[b, 0, u, f, at, :])
                 im = decode(hr[b, 1, u, f, at, :])
                 if it == 0:
-                    re = re + initial[0, b, u, f, at, :]
-                    im = im + initial[1, b, u, f, at, :]
+                    re = re + initial[0, b, l, at, :]
+                    im = im + initial[1, b, l, at, :]
                 x.append((re * (1.0 / RADIX), im * (1.0 / RADIX)))
             y = eight(x, 1)
             for t in range(RADIX):
@@ -386,9 +403,9 @@
                 work[0, f, t, at, :] = v[0]
                 work[1, f, t, at, :] = v[1]
 
-        loop(0, R // rows, some)
-
-    def stage_time(it):
+        loop(p * blocks, p * blocks + blocks, some)
+
+    def stage_time(it, p):
         def some(g):
             at = pl.ds(pl.multiple_of(g * rows, rows), rows)
 
@@ -409,12 +426,15 @@
 
             loop(0, RADIX, one)
 
-        loop(0, R // rows, some)
-
-    def own_out(f):
-        return pltpu.make_async_copy(gs.at[a, :, :, f], out.at[:, :, f, :, mine], out_sem.at[f])
-
-    def stage_out(it, f):
+        loop(p * blocks, p * blocks + blocks, some)
+
+    def own_out(part, m, p):
+        at, pair = strip(p), pl.ds(m * 2, 2)
+        return pltpu.make_async_copy(
+            gs.at[a, part, :, pair, at], (out_r, out_i)[part].at[:, pair, at, mine], out_sem.at[part, m * halves + p]
+        )
+
+    def stage_out(it, f, p):
         def some(g):
             at = pl.ds(pl.multiple_of(g * rows, rows), rows)
             y = eight([(work[0, f, t, at, :], work[1, f, t, at, :]) for t in range(RADIX)], -1)
@@ -424,15 +444,25 @@
                     v = y[f2][part] * (1.0 / RADIX)
                     gs[b, part, u, f, at, :] = v.astype(jnp.bfloat16) if it == 0 else encode(v)
 
-        loop(0, R // rows, some)
+        loop(p * blocks, p * blocks + blocks, some)
+
+    def give_back(f):
+        for p in range(halves):
+            stage_out(0, f, p)
         for j in range(1, A):
-            g_copy(it, j, f).start()
-        if it == 0:
-            for part in range(2):
-                for u in range(U):
-                    gr[part, u, f, :, mine] = gs[a, part, u, f]
-        else:
-            own_out(f).start()
+            g_copy(j, f).start()
+        for part in range(2):
+            for u in range(U):
+                gr[part, u, f, :, mine] = gs[a, part, u, f]
+
+    def give_out(m, p):
+        stage_out(1, 2 * m, p)
+        stage_out(1, 2 * m + 1, p)
+        for j in range(1, A):
+            o_copy(0, j, m, p).start()
+            o_copy(1, j, m, p).start()
+        for part in range(2):
+            own_out(part, m, p).start()
 
     for copy in locals_[:2] + locals_[4:]:
         copy.wait()
@@ -446,73 +476,74 @@
             arrive(far, h)
             loop(0, C, lambda chip: across_in(chip, h).wait_recv())
 
+        def slot(i):
+            n = h * per * U + i
+            if lent:
+
+                @pl.when(is_helper & (n >= F0 * U))
+                def _():
+                    lent_product(0, n - F0 * U)
+
+                @pl.when(is_end & (n >= F0 * U))
+                def _():
+                    returned(0, n - F0 * U)
+
+            @pl.when(keeps(h))
+            def _():
+                product(0, place(n))
+
+            @pl.when((n >= U) & (lax.rem(n, U) == U - 1))
+            def _():
+                for p in range(halves):
+                    stage_in(0, n // U - 1, p)
+
+        loop(0, per * U, slot)
+
+    loop(0, chunks, last)
+    for p in range(halves):
+        stage_in(0, RADIX - 1, p)
+    order = lambda i: lax.rem(F0 + i, RADIX)
+
+    loop(0, halves, lambda p: stage_time(0, p))
+    loop(0, RADIX, lambda i: give_back(order(i)))
+
+    def h_sent(f):
+        for p in range(halves):
+            for j in range(1, A):
+                h_copy(j, f, p).wait_send()
+
+    loop(0, RADIX, h_sent)
+
+    def again(i):
+        n = lax.rem(F0 * U + i, L)
+        l = place(n)
+
+        @pl.when(lax.rem(n, U) == 0)
+        def _():
+            for j in range(1, A):
+                g_copy_in(j, n // U).wait_recv()
+
         if lent:
-
-            @pl.when(is_helper & (h >= kept))
+            lends = is_end & (n >= F0 * U)
+
+            @pl.when(lends)
             def _():
-                loop(0, per, lambda i: lent_product(0, (h - kept) * per + i))
-
-            @pl.when(is_end & (h >= kept))
+                lend_g(n - F0 * U).start()
+
+            @pl.when(jnp.logical_not(lends))
             def _():
-                loop(0, per, lambda i: returned((h - kept) * per + i))
-
-        @pl.when(keeps(h))
-        def _():
-            loop(0, per, lambda i: product(0, h * per + i))
-
-        @pl.when(h > 0)
-        def _():
-            loop(0, per, lambda i: stage_in(0, (h - 1) * per + i))
-
-    loop(0, chunks, last)
-    loop(0, per, lambda i: stage_in(0, (chunks - 1) * per + i))
-    stage_time(0)
-    order = lambda i: lax.rem(F0 + i, RADIX)
-    loop(0, RADIX, lambda i: stage_out(0, order(i)))
-
-    def h_sent(f):
-        for j in range(1, A):
-            h_copy(j, f).wait_send()
-
-    loop(0, RADIX, h_sent)
-
-    def lends(f):
-        return is_end & (f >= F0)
-
-    def again(i):
-        f = order(i)
-        for j in range(1, A):
-            g_copy_in(0, j, f).wait_recv()
-        if lent:
-
-            @pl.when(lends(f))
+                product(1, l)
+
+            @pl.when(is_helper & (i >= LAG) & (lax.rem(i, 2) == 0) & (i < 2 * Q + LAG))
             def _():
-                lend_g(f - F0).start()
-
-            @pl.when(jnp.logical_not(lends(f)))
-            def _():
-                product(1, f)
-
-            @pl.when(is_helper & (i >= 2) & (lax.rem(i, 2) == 0) & (i < 2 * Q + 2))
-            def _():
-                lent_product(1, i // 2 - 1)
-
-            before = order(i + RADIX - 1)
-
-            @pl.when((i > 0) & jnp.logical_not(lends(before)))
-            def _():
-                stage_in(1, before)
+                lent_product(1, (i - LAG) // 2)
 
         else:
-            product(1, f)
-
-            @pl.when(i > 0)
-            def _():
-                stage_in(1, order(i + RADIX - 1))
-
-    loop(0, RADIX, again)
+            product(1, l)
+
+    loop(0, L, again)
     if lent:
-        late = (RADIX - 1) // 2
+        late = (L - LAG + 1) // 2
 
         @pl.when(is_helper)
         def _():
@@ -521,8 +552,15 @@
 
         @pl.when(is_end)
         def _():
-            loop(0, Q, returned)
-
+            loop(0, Q, lambda n: returned(1, n))
+
+
+    def rest(f):
+        for p in range(1, halves):
+            for j in range(1, A):
+                h_copy(j, f, p).start()
+
+    loop(0, RADIX, rest)
     by_af[a] = squares[...]
 
     def af_copy(j):
@@ -533,18 +571,19 @@
 
     for j in range(1, A):
         af_copy(j).start()
-    stage_in(1, order(RADIX - 1))
-    if lent:
-
-        @pl.when(is_end)
-        def _():
-            loop(0, Q, lambda n: stage_in(1, F0 + n))
-
-    stage_time(1)
-    for j in range(1, A):
-        g_sent = lambda f: g_copy(0, j, f).wait_send()
-        loop(0, RADIX, g_sent)
-    loop(0, RADIX, lambda f: stage_out(1, f))
+
+    def g_sent(f):
+        for j in range(1, A):
+            g_copy(j, f).wait_send()
+
+    loop(0, RADIX, g_sent)
+
+    def turn_over(p):
+        loop(0, RADIX, lambda i: stage_in(1, order(i + RADIX - F0), p))
+        stage_time(1, p)
+        loop(0, RADIX // 2, lambda m: give_out(m, p))
+
+    loop(0, halves, turn_over)
 
     for j in range(1, A):
         af_copy_in(j).wait_recv()
@@ -600,13 +639,15 @@
         mis[it] = jnp.sum(full[it]) * (1.0 / (U * RADIX * A * N * N))
     loop(1, S, lambda j: sa_copy(j).wait_send())
 
-    def finish(f):
-        for j in range(1, A):
-            g_copy_in(1, j, f).wait_recv()
-            g_copy(1, j, f).wait_send()
-        own_out(f).wait()
-
-    loop(0, RADIX, finish)
+    def finish(m):
+        for p in range(halves):
+            for j in range(1, A):
+                o_both(j, m, p).wait_recv()
+                o_both(j, m, p).wait_send()
+            for part in range(2):
+                own_out(part, m, p).wait()
+
+    loop(0, RADIX // 2, finish)
 
 
 def on_device(counts, data_real, data_imaginary, wave_real, wave_imaginary, primaries_real, primaries_imaginary):
@@ -616,27 +657,29 @@
     W = N // A
     U = L // RADIX
     chunks = RADIX if C <= 8 else 1
-    lent = LENT if C >= 4 and chunks > LENT else 0
-    Q = max(1, lent * RADIX // chunks)
+    halves = 2 if R % 32 == 0 else 1
+    split = lambda v: v.reshape(U, RADIX, R, N)
+    kept = RADIX - LENT if C >= 4 and chunks > 1 else RADIX
+    Q = max(1, (RADIX - kept) * U)
     turns = 2 * np.pi * np.arange(RADIX * RADIX) / (RADIX * RADIX)
     twiddle = jnp.asarray(np.stack([np.cos(turns), np.sin(turns)]), jnp.float32)
     smem = pl.BlockSpec(memory_space=pltpu.SMEM)
     hbm = pl.BlockSpec(memory_space=pl.ANY)
     f32, bf16 = jnp.float32, jnp.bfloat16
     dma = pltpu.SemaphoreType.DMA
-    split = lambda v: v.reshape(U, RADIX, R, N)
-    coded, misfit = pl.pallas_call(
-        functools.partial(kernel, A, S, chunks, lent),
+    coded_r, coded_i, misfit = pl.pallas_call(
+        functools.partial(kernel, A, S, chunks, kept),
         in_specs=[smem, smem, smem, hbm, hbm, hbm, hbm],
-        out_specs=[hbm, smem],
+        out_specs=[hbm, hbm, smem],
         out_shape=[
-            jax.ShapeDtypeStruct((2, U, RADIX, R, N), bf16),
+            jax.ShapeDtypeStruct((U, RADIX, R, N), bf16),
+            jax.ShapeDtypeStruct((U, RADIX, R, N), bf16),
             jax.ShapeDtypeStruct((ITERS,), f32),
         ],
         scratch_shapes=[
             pltpu.VMEM((U, RADIX, 2, S, R, N), bf16),
-            pltpu.VMEM((2, U, RADIX, R, N), f32),
-            pltpu.VMEM((2, A, U, RADIX, R, W), f32),
+            pltpu.VMEM((2, L, R, N), f32),
+            pltpu.VMEM((2, A, L, R, W), f32),
             pltpu.VMEM((2, RADIX, RADIX, R, W), f32),
             pltpu.VMEM((2, RADIX, RADIX, R, W), f32),
             pltpu.VMEM((A, 2, U, RADIX, R, W), bf16),
@@ -646,8 +689,8 @@
             pltpu.VMEM((ITERS, 8, 128), f32),
             pltpu.VMEM((A, ITERS, 8, 128), f32),
             pltpu.VMEM((S, ITERS, 8, 128), f32),
-            pltpu.VMEM((2, U, Q, R, N), bf16),
-            pltpu.VMEM((A, 2, U, Q, R, W), bf16),
+            pltpu.VMEM((2, Q, R, N), bf16),
+            pltpu.VMEM((A, 2, Q, R, W), bf16),
             dma((6,)),
             dma((C, chunks)),
             dma((C, chunks)),
@@ -656,27 +699,28 @@
             dma((C, chunks)),
             dma((2, A)),
             dma((2, A)),
+            dma((A, RADIX * halves)),
+            dma((A, RADIX * halves)),
             dma((A, RADIX)),
             dma((A, RADIX)),
-            dma((ITERS, A, RADIX)),
-            dma((ITERS, A, RADIX)),
+            dma((A, RADIX * halves // 2)),
+            dma((A, RADIX * halves // 2)),
             dma((A + S,)),
             dma((A + S,)),
             dma((Q,)),
             dma((Q,)),
             dma((Q,)),
             dma((Q,)),
-            dma((RADIX,)),
+            dma((2, RADIX * halves // 2)),
         ],
         compiler_params=pltpu.CompilerParams(
             collective_id=0, has_side_effects=True, vmem_limit_bytes=63 * 2**20
         ),
     )(
         wave_real, wave_imaginary, twiddle,
-        split(data_real), split(data_imaginary), split(primaries_real), split(primaries_imaginary),
+        split(data_real), split(data_imaginary), primaries_real, primaries_imaginary,
     )
-    updated = [decode(coded[part]).reshape(L, R, N) for part in range(2)]
-    return (updated[0], updated[1], misfit)
+    return (decode(coded_r).reshape(L, R, N), decode(coded_i).reshape(L, R, N), misfit)
 
 
 def solution(mesh):

time: 201 us -> 196 us (0.975)
  Pallas kernels: 195 us -> 190 us
    pallas_call x1, Pallas kernels: 195 us -> 190 us  [on_device(): pl.pallas_call(functools.partial(kernel, A, S, chunks, kept), in_specs=[s...]
where the time goes in v4:
time: 196 us
  Pallas kernels  190 us (97%)
  other arithmetic  4.77 us (2%)
    pallas_call x1, Pallas kernels, on_device(): pl.pallas_call(functools.partial(kernel, A, S, chunks, kept), in_specs=[s...  190 us
    mul x1, other arithmetic, decode(): return v * y * y * (lax.rsqrt(y) * REACH)  4.77 us

profile of v4, /device:TPU:0, one launch (start us, length us, event | category | flops | bytes accessed | tf_op | source)
XLA Modules:
  0.0 195.7 jit_solution(6971127440057397748)
XLA Ops:
  0.6 189.8 %shard_map.94 = (bf16[2,8,64,512]{3,2,1,0:T(8,128)(2,1)}, bf16[2,8,64,512]{3,2,1,0:T(8,128)(2,1)}, f32[2]{0:T(128)}) custom-call(f32[16]{0:T(128)} %wr.1, f32[16]{0:T(128)} %wi.1, f32[2,64]{1,0:T(2,128)} %constant.6.clone.twiddle, bf16[2,8,64,512]{3,2,1,0:T(8,128)(2,1)} %bitcast.6, bf16[2,8,64,512]{3,2,1,0:T(8,128)(2,1)} %bitcast.7, f32[16,64,512]{2,1,0:T(8,128)} %prim_r.1, ...), custom_call_target="tpu_custom_call" | custom-call | tf_op jit(solution)/shard_map/pallas_call | solution.py:670
  190.4 0.0 copy-start
  190.4 4.8 %fusion.4 = (f32[2,8,64,512]{3,2,1,0:T(8,128)}, f32[2,8,64,512]{3,2,1,0:T(8,128)}) fusion(bf16[2,8,64,512]{3,2,1,0:T(8,128)(2,1)} %get-tuple-element.6, bf16[2,8,64,512]{3,2,1,0:T(8,128)(2,1)} %get-tuple-element.7), kind=kLoop, calls=%fused_computation.8 | loop fusion | flops 7340032 | bytes 6291456 | tf_op jit(solution)/shard_map/mul | solution.py:32
  195.2 0.0 copy-done
  195.2 0.5 copy.11
Async XLA Ops:
  190.4 4.8 %copy-start = (f32[2]{0:T(128)S(1)}, f32[2]{0:T(128)}, u32[]{:S(2)}) copy-start(f32[2]{0:T(128)} %get-tuple-element.16) | copy-start | bytes 28

commit v5 on v4

--- a/solution.py
+++ b/solution.py
@@ -665,6 +665,7 @@
     twiddle = jnp.asarray(np.stack([np.cos(turns), np.sin(turns)]), jnp.float32)
     smem = pl.BlockSpec(memory_space=pltpu.SMEM)
     hbm = pl.BlockSpec(memory_space=pl.ANY)
+    vmem = pl.BlockSpec(memory_space=pltpu.VMEM)
     f32, bf16 = jnp.float32, jnp.bfloat16
     dma = pltpu.SemaphoreType.DMA
     coded_r, coded_i, misfit = pl.pallas_call(
@@ -672,8 +673,8 @@
         in_specs=[smem, smem, smem, hbm, hbm, hbm, hbm],
         out_specs=[hbm, hbm, smem],
         out_shape=[
-            jax.ShapeDtypeStruct((U, RADIX, R, N), bf16),
-            jax.ShapeDtypeStruct((U, RADIX, R, N), bf16),
+            pltpu.VMEM((U, RADIX, R, N), bf16),
+            pltpu.VMEM((U, RADIX, R, N), bf16),
             jax.ShapeDtypeStruct((ITERS,), f32),
         ],
         scratch_shapes=[
@@ -714,7 +715,7 @@
             dma((2, RADIX * halves // 2)),
         ],
         compiler_params=pltpu.CompilerParams(
-            collective_id=0, has_side_effects=True, vmem_limit_bytes=63 * 2**20
+            collective_id=0, has_side_effects=True, vmem_limit_bytes=61 * 2**20
         ),
     )(
         wave_real, wave_imaginary, twiddle,

time: 196 us -> 194 us (0.990)
  no operation moved by 1% of the time
where the time goes in v5:
time: 194 us
  Pallas kernels  190 us (98%)
  other arithmetic  3.23 us (2%)
    pallas_call x1, Pallas kernels, on_device(): pl.pallas_call(functools.partial(kernel, A, S, chunks, kept), in_specs=[s...  190 us

profile of v5, /device:TPU:0, one launch (start us, length us, event | category | flops | bytes accessed | tf_op | source)
XLA Modules:
  0.0 194.1 jit_solution(5182659052998631204)
XLA Ops:
  0.6 189.7 %shard_map.94 = (bf16[2,8,64,512]{3,2,1,0:T(8,128)(2,1)S(1)}, bf16[2,8,64,512]{3,2,1,0:T(8,128)(2,1)S(1)}, f32[2]{0:T(128)}) custom-call(f32[16]{0:T(128)} %wr.1, f32[16]{0:T(128)} %wi.1, f32[2,64]{1,0:T(2,128)} %constant.6.clone.twiddle, bf16[2,8,64,512]{3,2,1,0:T(8,128)(2,1)} %bitcast.6, bf16[2,8,64,512]{3,2,1,0:T(8,128)(2,1)} %bitcast.7, ...), custom_call_target="tpu_custom_call" | custom-call | tf_op jit(solution)/shard_map/pallas_call | solution.py:671
  190.3 0.0 copy-start
  190.3 3.2 %fusion.4 = (f32[2,8,64,512]{3,2,1,0:T(8,128)}, f32[2,8,64,512]{3,2,1,0:T(8,128)}) fusion(bf16[2,8,64,512]{3,2,1,0:T(8,128)(2,1)S(1)} %get-tuple-element.6, bf16[2,8,64,512]{3,2,1,0:T(8,128)(2,1)S(1)} %get-tuple-element.7), kind=kLoop, calls=%fused_computation.8 | loop fusion | flops 7340032 | bytes 6291456 | tf_op jit(solution)/shard_map/mul | solution.py:32
  193.6 0.0 copy-done
  193.6 0.5 copy.11
Async XLA Ops:
  190.3 3.2 %copy-start = (f32[2]{0:T(128)S(1)}, f32[2]{0:T(128)}, u32[]{:S(2)}) copy-start(f32[2]{0:T(128)} %get-tuple-element.16) | copy-start | bytes 28

commit v6 on v5

--- a/solution.py
+++ b/solution.py
@@ -79,7 +79,7 @@
     whole, current, initial, work, traces, hs, hr, gs, gr, squares, by_af, by_sa, lent_g, lent_h,
     local_sem, up_sem, down_sem, ring_sem, pair_send, pair_recv,
     init_send, init_recv, h_send, h_recv, g_send, g_recv, o_send, o_recv, m_send, m_recv,
-    lg_send, lg_recv, lh_send, lh_recv, out_sem,
+    lg_send, lg_recv, lh_send, lh_recv, d_send, d_recv, out_sem,
 ):
     C = S // 2
     L, R, N = prim_r.shape
@@ -101,6 +101,7 @@
         is_end = (c == 0) | (c == C - 1)
         is_helper = (c == 1) | (c == C - 2)
         other = jnp.where((c == 0) | (c == C - 2), s + 2, s - 2)
+        lender = is_end | is_helper
 
     def goes_up(h):
         go = c + 1 < C
@@ -134,6 +135,16 @@
         1, S,
         lambda j: pl.semaphore_signal(barrier, inc=1, device_id=(a, lax.rem(s + j, S)), device_id_type=MESH),
     )
+
+    greeted = A - 1 + S - 1
+    if lent:
+
+        @pl.when(lender)
+        def _():
+            for j in range(1, A):
+                pl.semaphore_signal(barrier, inc=1, device_id=(ahead(j), other), device_id_type=MESH)
+
+        greeted = greeted + jnp.where(lender, A - 1, 0)
 
     locals_ = [
         pltpu.make_async_copy(data_r, whole.at[:, :, 0, s], local_sem.at[0]),
@@ -146,7 +157,7 @@
     for copy in locals_:
         copy.start()
     squares[...] = jnp.zeros_like(squares)
-    pl.semaphore_wait(barrier, A - 1 + S - 1)
+    pl.semaphore_wait(barrier, greeted)
 
     def shard(chip, core, h):
         return whole.at[:, pl.ds(h * per, per), :, chip * 2 + core]
@@ -224,6 +235,9 @@
 
     def lend_g(n):
         return remote(gr.at[:, lax.rem(n, U), F0 + n // U], lent_g.at[:, n], lg_send.at[n], lg_recv.at[n], (a, other))
+
+    def lend_first(n):
+        return remote(lent_g.at[:, n], lent_g.at[:, n], lg_send.at[n], lg_recv.at[n], (a, other))
 
     def lend_h(n):
         return remote(lent_h.at[:, :, n], hs.at[:, :, lax.rem(n, U), F0 + n // U], lh_send.at[n], lh_recv.at[n], (a, other))
@@ -240,8 +254,8 @@
             def lend(n):
                 at = place(F0 * U + n)
                 for part in range(2):
-                    gr[part, lax.rem(n, U), F0 + n // U] = current[part, at].astype(jnp.bfloat16)
-                lend_g(n).start()
+                    lent_g[part, n] = current[part, at].astype(jnp.bfloat16)
+                lend_first(n).start()
 
             loop(0, Q, lend)
 
@@ -339,6 +353,18 @@
         di = encode(STEP_LENGTH * (qr * ei - qi * er - (br[R:] - bi[:R])))
         return dr, di
 
+    def direct(j, n):
+        to = ahead(j)
+        return remote(
+            lent_h.at[to, :, n], hr.at[a, :, lax.rem(n, U), F0 + n // U], d_send.at[j, n], d_recv.at[j, n], (to, other)
+        )
+
+    def direct_in(j, n):
+        return remote(
+            lent_h.at[a, :, n], hr.at[behind(j), :, lax.rem(n, U), F0 + n // U],
+            d_send.at[j, n], d_recv.at[j, n], (ahead(j), other),
+        )
+
     def publish(it, l):
         u, f = l // RADIX, lax.rem(l, RADIX)
         hr[a, 0, u, f] = hs[a, 0, u, f]
@@ -365,14 +391,19 @@
     def lent_product(it, n):
         lend_g(n).wait_recv()
         if it > 0:
-            lend_h(n).wait_send()
+            for j in range(A):
+                direct(j, n).wait_send()
         dr, di = step_of(
             it, place(F0 * U + n), other, lent_g[0, n].astype(jnp.float32), lent_g[1, n].astype(jnp.float32)
         )
         for b in range(A):
             lent_h[b, 0, n] = dr[:, b * W : (b + 1) * W]
             lent_h[b, 1, n] = di[:, b * W : (b + 1) * W]
-        lend_h(n).start()
+        if it > 0:
+            lend_h(n).start()
+        else:
+            for j in range(A):
+                direct(j, n).start()
 
     def returned(it, n):
         lend_h(n).wait_recv()
@@ -382,8 +413,25 @@
     blocks = half // rows
 
     def stage_in(it, f, p):
-        for j in range(1, A):
-            h_copy_in(j, f, p).wait_recv()
+        if lent and it == 0:
+            by_lender = is_end & (f >= F0)
+
+            @pl.when(by_lender & (p == 0))
+            def _():
+                for u in range(U):
+                    n = (f - F0) * U + u
+                    lend_first(n).wait_send()
+                    for j in range(A):
+                        direct_in(j, n).wait_recv()
+
+            @pl.when(jnp.logical_not(by_lender))
+            def _():
+                for j in range(1, A):
+                    h_copy_in(j, f, p).wait_recv()
+
+        else:
+            for j in range(1, A):
+                h_copy_in(j, f, p).wait_recv()
 
         def some(g):
             at = pl.ds(pl.multiple_of(g * rows, rows), rows)
@@ -484,10 +532,6 @@
                 def _():
                     lent_product(0, n - F0 * U)
 
-                @pl.when(is_end & (n >= F0 * U))
-                def _():
-                    returned(0, n - F0 * U)
-
             @pl.when(keeps(h))
             def _():
                 product(0, place(n))
@@ -512,7 +556,7 @@
             for j in range(1, A):
                 h_copy(j, f, p).wait_send()
 
-    loop(0, RADIX, h_sent)
+    loop(0, jnp.where(is_end, F0, RADIX) if lent else RADIX, h_sent)
 
     def again(i):
         n = lax.rem(F0 * U + i, L)
@@ -712,6 +756,8 @@
             dma((Q,)),
             dma((Q,)),
             dma((Q,)),
+            dma((A, Q)),
+            dma((A, Q)),
             dma((2, RADIX * halves // 2)),
         ],
         compiler_params=pltpu.CompilerParams(

time: 194 us -> 193 us (level)
  Pallas kernels: 190 us -> 188 us
where the time goes in v6:
time: 193 us; the launch traced here: 192 us
  Pallas kernels  188 us (97%)
  other arithmetic  3.23 us (2%)
    pallas_call x1, Pallas kernels, on_device(): pl.pallas_call(functools.partial(kernel, A, S, chunks, kept), in_specs=[s...  188 us

profile of v6, /device:TPU:0, one launch (start us, length us, event | category | flops | bytes accessed | tf_op | source)
XLA Modules:
  0.0 192.4 jit_solution(17971256652533008254)
XLA Ops:
  0.6 188.0 %shard_map.94 = (bf16[2,8,64,512]{3,2,1,0:T(8,128)(2,1)S(1)}, bf16[2,8,64,512]{3,2,1,0:T(8,128)(2,1)S(1)}, f32[2]{0:T(128)}) custom-call(f32[16]{0:T(128)} %wr.1, f32[16]{0:T(128)} %wi.1, f32[2,64]{1,0:T(2,128)} %constant.6.clone.twiddle, bf16[2,8,64,512]{3,2,1,0:T(8,128)(2,1)} %bitcast.6, bf16[2,8,64,512]{3,2,1,0:T(8,128)(2,1)} %bitcast.7, ...), custom_call_target="tpu_custom_call" | custom-call | tf_op jit(solution)/shard_map/pallas_call | solution.py:715
  188.6 0.0 copy-start
  188.6 3.2 %fusion.4 = (f32[2,8,64,512]{3,2,1,0:T(8,128)}, f32[2,8,64,512]{3,2,1,0:T(8,128)}) fusion(bf16[2,8,64,512]{3,2,1,0:T(8,128)(2,1)S(1)} %get-tuple-element.6, bf16[2,8,64,512]{3,2,1,0:T(8,128)(2,1)S(1)} %get-tuple-element.7), kind=kLoop, calls=%fused_computation.8 | loop fusion | flops 7340032 | bytes 6291456 | tf_op jit(solution)/shard_map/mul | solution.py:32
  191.9 0.0 copy-done
  191.9 0.5 copy.11
Async XLA Ops:
  188.6 3.2 %copy-start = (f32[2]{0:T(128)S(1)}, f32[2]{0:T(128)}, u32[]{:S(2)}) copy-start(f32[2]{0:T(128)} %get-tuple-element.16) | copy-start | bytes 28
